TPU v7x, 32 devices: a whole 2x2x4 slice. The times are simulated.
32 devices in a mesh: gx: 4 (over z), gy: 4 (over y, x), gz: 2 (over core).
Axes of the slice: x: 2, y: 2, z: 4, core: 2. Of those that a mesh axis runs over, the one named last changes fastest.
Arguments:
- eigvecs: bfloat16 [64, 32, 96, 512], P('gx', 'gy', 'gz'), may hold values from -7 to 7, as said below
- material: float32 [2, 64, 32, 96], P(None, 'gx', 'gy', 'gz'), may hold values from 0.5 to 2
Outputs:
- stiffness: float32 [512, 512], P(('gx', 'gy', 'gz'))
- mass_matrix: float32 [512, 512], P(('gx', 'gy', 'gz'))
Inputs may be any that keep to these rules, and one draw needn't show every extreme that they name: `eigvecs`: entries are a rough part plus a part that varies slowly over the grid.
All inputs are finite; a program needn't handle non-finite values.
Results may differ from a plain program's by a relative error of at most 0.0003.
Values may be sent and summed in bfloat16 or wider, within the bound.
A program may use at most 128 MiB of HBM per device.

v0:
```python
import jax
import jax.numpy as jnp
from jax import lax
from jax.sharding import PartitionSpec as P

corner_weight = 0.0625
coupling_total = 3.5
mass_side = 1.0 / 6.0
mass_middle = 4.0 / 6.0


def with_halo(cells, sides, width):
    for axis, dim in sides:
        count = lax.axis_size(axis)
        ends = count - 1
        head = lax.slice_in_dim(cells, 0, width, axis=dim)
        tail = lax.slice_in_dim(cells, cells.shape[dim] - width, cells.shape[dim], axis=dim)
        cells = jnp.concatenate(
            [
                lax.ppermute(tail, axis, [(i, (i + 1) % count) for i in range(ends)]),
                cells,
                lax.ppermute(head, axis, [((i + 1) % count, i) for i in range(ends)]),
            ],
            axis=dim,
        )
    return cells


def three_taps(field, side, middle):
    for axis_dim in (0, 1, 2):
        inner = field.shape[axis_dim] - 2
        lower = lax.slice_in_dim(field, 0, inner, axis=axis_dim)
        centre = lax.slice_in_dim(field, 1, inner + 1, axis=axis_dim)
        upper = lax.slice_in_dim(field, 2, inner + 2, axis=axis_dim)
        field = side * (lower + upper) + middle * centre
    return field


def apply_operators(padded, padded_material):
    values = padded.astype(jnp.float32)
    kappa = padded_material[0]
    rho = padded_material[1]
    centre = values[1:-1, 1:-1, 1:-1]
    kappa_centre = kappa[1:-1, 1:-1, 1:-1]
    rho_centre = rho[1:-1, 1:-1, 1:-1]
    kappa_values = kappa[..., None] * values
    rho_values = rho[..., None] * values
    self_weight = 8.0 * corner_weight
    near_values = corner_weight * three_taps(values, 1.0, 2.0) - self_weight * centre
    near_kappa_values = (
        corner_weight * three_taps(kappa_values, 1.0, 2.0)
        - self_weight * kappa_values[1:-1, 1:-1, 1:-1]
    )
    near_kappa = corner_weight * three_taps(kappa, 1.0, 2.0) - self_weight * kappa_centre
    row_weight = 0.5 * (coupling_total * kappa_centre + near_kappa)
    stiff_sum = (
        row_weight[..., None] * centre
        - 0.5 * kappa_centre[..., None] * near_values
        - 0.5 * near_kappa_values
    )
    mass_sum = 0.5 * rho_centre[..., None] * three_taps(
        values, mass_side, mass_middle
    ) + 0.5 * three_taps(rho_values, mass_side, mass_middle)
    return (stiff_sum.astype(jnp.bfloat16), mass_sum.astype(jnp.bfloat16))


def per_device(eigvecs, material):
    size_x, size_y, size_z, columns = eigvecs.shape
    cells = size_x * size_y * size_z
    block_cols = 128
    padded_material = with_halo(material, (("gx", 1), ("gy", 2), ("gz", 3)), 1)
    padded = with_halo(eigvecs, (("gx", 0), ("gy", 1), ("gz", 2)), 1)

    def column_block(block_index):
        col_block = lax.dynamic_slice_in_dim(padded, block_index * block_cols, block_cols, 3)
        stiff_vecs, mass_vecs = apply_operators(col_block, padded_material)
        return (stiff_vecs.reshape(cells, block_cols), mass_vecs.reshape(cells, block_cols))

    stiff_blocks, mass_blocks = lax.map(
        column_block, jnp.arange(columns // block_cols, dtype=jnp.int32)
    )
    flat_vectors = eigvecs.reshape(cells, columns)
    devices_all = lax.axis_size("gx") * lax.axis_size("gy") * lax.axis_size("gz")
    total_cells = cells * devices_all
    row_count = columns // lax.axis_size("gx") * lax.axis_size("gx")
    stiff_part = jnp.einsum(
        "cp,bcq->pbq", flat_vectors, stiff_blocks, preferred_element_type=jnp.float32
    ).reshape(row_count, columns)
    mass_part = jnp.einsum(
        "cp,bcq->pbq", flat_vectors, mass_blocks, preferred_element_type=jnp.float32
    ).reshape(row_count, columns)
    section_one = lax.psum_scatter(
        jnp.concatenate([stiff_part, mass_part], axis=1), "gx", scatter_dimension=0, tiled=True
    )
    section_two = lax.psum_scatter(section_one, "gy", scatter_dimension=0, tiled=True)
    summed = lax.psum_scatter(section_two, "gz", scatter_dimension=0, tiled=True)
    stiffness = summed[:, :columns] / total_cells
    mass_matrix = summed[:, columns:] / total_cells
    return (stiffness, mass_matrix)


def solution(mesh):
    return jax.shard_map(
        per_device,
        mesh=mesh,
        in_specs=(P("gx", "gy", "gz", None), P(None, "gx", "gy", "gz")),
        out_specs=(P(("gx", "gy", "gz"), None), P(("gx", "gy", "gz"), None)),
        check_vma=False,
    )
```

profile of v0, /device:TPU:0, one launch (start us, length us, event | category | flops | bytes accessed | tf_op | source)
XLA Modules:
  0.0 324.0 jit_solution(1531732146435684193)
XLA Ops:
  8.4 5.0 %collective-permute-start.6 = (bf16[1,8,48,512]{3,2,1,0:T(8,128)(2,1)S(1)}, bf16[1,8,48,512]{3,2,1,0:T(8,128)(2,1)S(1)}, u32[]{:S(2)}, u32[]{:S(2)}) collective-permute-start(bf16[1,8,48,512]{3,2,1,0:T(8,128)(2,1)S(1)} %get-tuple-element.95), channel_id=1, source_target_pairs={{0,8},{8,16},{16,24},{1,9},{9,17},{17,25},{2,10},{10,18},{18,26},{... | collective-permute-start | bytes 1179656 | tf_op jit(solution)/shard_map/ppermute | solution.py:20
  14.1 3.4 %collective-permute-start = (f32[2,1,8,48]{3,2,1,0:T(8,128)S(1)}, f32[2,1,8,48]{3,2,1,0:T(8,128)S(1)}, u32[]{:S(2)}, u32[]{:S(2)}) collective-permute-start(f32[2,1,8,48]{3,2,1,0:T(8,128)S(1)} %get-tuple-element.101), channel_id=1, source_target_pairs={{0,8},{8,16},{16,24},{1,9},{9,17},{17,25},{2,10},{10,18},{18,26},{... | collective-permute-start | bytes 9224 | tf_op jit(solution)/shard_map/ppermute | solution.py:20
  20.1 1.7 collective-permute-done
  21.9 3.9 %constant_dynamic-update-slice_fusion.6 = bf16[18,8,48,512]{3,2,1,0:T(8,128)(2,1)S(1)} fusion(bf16[18,8,48,512]{3,2,1,0:T(8,128)(2,1)S(1)} %constant_dynamic-update-slice_fusion.7, bf16[16,8,48,512]{3,2,1,0:T(8,128)(2,1)} %param.4), kind=kLoop, calls=%fused_computation.87 | loop fusion | bytes 12582912
  25.8 5.9 %collective-permute-done.7 = bf16[1,8,48,512]{3,2,1,0:T(8,128)(2,1)S(1)} collective-permute-done((bf16[1,8,48,512]{3,2,1,0:T(8,128)(2,1)S(1)}, bf16[1,8,48,512]{3,2,1,0:T(8,128)(2,1)S(1)}, u32[]{:S(2)}, u32[]{:S(2)}) %collective-permute-start.7) | collective-permute-done | bytes 393248 | tf_op jit(solution)/shard_map/ppermute | solution.py:22
  31.7 2.9 copy-done.1
  37.3 5.5 %collective-permute-start.8 = (bf16[18,1,48,512]{3,2,1,0:T(8,128)(2,1)}, bf16[18,1,48,512]{3,2,1,0:T(8,128)(2,1)}, u32[]{:S(2)}, u32[]{:S(2)}) collective-permute-start(bf16[18,1,48,512]{3,2,1,0:T(8,128)(2,1)} %get-tuple-element.92), channel_id=1, source_target_pairs={{0,2},{2,4},{4,6},{1,3},{3,5},{5,7},{8,10},{10,12},{12,14},{9,11},... | collective-permute-start | bytes 2654216 | tf_op jit(solution)/shard_map/ppermute | solution.py:20
  42.9 1.6 collective-permute-start.3
  44.4 4.5 %collective-permute-start.2 = (f32[2,18,1,48]{3,2,1,0:T(1,128)S(1)}, f32[2,18,1,48]{3,2,1,0:T(1,128)S(1)}, u32[]{:S(2)}, u32[]{:S(2)}) collective-permute-start(f32[2,18,1,48]{3,2,1,0:T(1,128)S(1)} %get-tuple-element.98), channel_id=1, source_target_pairs={{0,2},{2,4},{4,6},{1,3},{3,5},{5,7},{8,10},{10,12},{12,14},{9,11},... | collective-permute-start | bytes 20744 | tf_op jit(solution)/shard_map/ppermute | solution.py:20
  49.0 28.6 %collective-permute-done.3 = f32[2,18,1,48]{3,2,1,0:T(1,128)S(1)} collective-permute-done((f32[2,18,1,48]{3,2,1,0:T(1,128)S(1)}, f32[2,18,1,48]{3,2,1,0:T(1,128)S(1)}, u32[]{:S(2)}, u32[]{:S(2)}) %collective-permute-start.3) | collective-permute-done | bytes 6944 | tf_op jit(solution)/shard_map/ppermute | solution.py:22
  79.9 3.8 %collective-permute-start.4 = (f32[2,18,10,1]{3,2,1,0:T(8,128)}, f32[2,18,10,1]{3,2,1,0:T(8,128)}, u32[]{:S(2)}, u32[]{:S(2)}) collective-permute-start(f32[2,18,10,1]{3,2,1,0:T(8,128)} %get-tuple-element.96), channel_id=1, source_target_pairs={{0,1},{2,3},{4,5},{6,7},{8,9},{10,11},{12,13},{14,15},{16,17},{18,... | collective-permute-start | bytes 4328 | tf_op jit(solution)/shard_map/ppermute | solution.py:20
  85.8 2.6 pad_maximum_fusion.4
  89.7 3.3 %collective-permute-start.10 = (bf16[18,10,1,512]{3,2,1,0:T(2,128)(2,1)S(1)}, bf16[18,10,1,512]{3,2,1,0:T(2,128)(2,1)S(1)}, u32[]{:S(2)}, u32[]{:S(2)}) collective-permute-start(bf16[18,10,1,512]{3,2,1,0:T(2,128)(2,1)S(1)} %get-tuple-element.90), channel_id=1, source_target_pairs={{0,1},{2,3},{4,5},{6,7},{8,9},{10,11},{12,13},{14,15},{16,17},{18,... | collective-permute-start | bytes 552968 | tf_op jit(solution)/shard_map/ppermute | solution.py:20
  94.1 9.4 %pad_maximum_fusion = bf16[18,10,50,512]{3,2,1,0:T(8,128)(2,1)} fusion(bf16[18,10,1,512]{3,2,1,0:T(2,128)(2,1)S(1)} %collective-permute-done.11, bf16[18,1,48,512]{3,2,1,0:T(8,128)(2,1)} %collective-permute-done.9, bf16[18,8,48,512]{3,2,1,0:T(8,128)(2,1)S(1)} %bitcast.39, bf16[18,1,48,512]{3,2,1,0:T(8,128)(2,1)} %collective-permute-done.8, ...), kind=kLoop, calls=%fused_computation.72 | loop fusion | flops 46080000 | bytes 18432000 | tf_op jit(solution)/shard_map/concatenate | solution.py:18
  103.5 114.3 %while.13 = (s32[]{:T(128)}, bf16[4,6144,128]{2,1,0:T(8,128)(2,1)}, bf16[4,6144,128]{2,1,0:T(8,128)(2,1)}, f32[2,18,10,50]{3,2,1,0:T(8,128)S(1)}, f32[16,10,50]{...) while((s32[]{:T(128)}, bf16[4,6144,128]{2,1,0:T(8,128)(2,1)}, ...), condition=%wide.region_1.2_spmd, body=%wide.region_0.1_spmd.sunk | while | flops 53078404 | bytes 184562576 | solution.py:79
  104.8 5.8 %broadcast_multiply_fusion.3 = (f32[18,10,50,128]{3,2,1,0:T(8,128)S(1)}, f32[18,10,50,128]{3,2,1,0:T(8,128)S(1)}) fusion(f32[18,10,50]{2,1,0:T(8,128)S(1)} %get-tuple-element.157, bf16[18,10,50,512]{3,2,1,0:T(8,128)(2,1)} %get-tuple-element.195, s32[]{:T(128)S(6)} %select_n.5, f32[18,10,50]{2,1,0:T(8,128)S(1)} %get-tuple-element.158), kind=kLoop, calls=%fused_computation.52.clone.1 | loop fusion | flops 3456000 | bytes 11592004 | tf_op jit(solution)/shard_map/while/body/eval_jaxpr/mul | solution.py:47
  111.7 2.1 dynamic-slice_convert_fusion.2
  113.8 2.8 multiply_add_fusion.3
  117.2 3.1 fusion.59
  121.3 5.1 %fusion.62 = f32[16,8,50,128]{3,2,1,0:T(8,128)S(1)} fusion(f32[16,10,50,128]{3,2,1,0:T(8,128)} %get-tuple-element.162), kind=kLoop, calls=%fused_computation.22.clone.1 | loop fusion | flops 2457600 | bytes 13107200 | tf_op jit(solution)/shard_map/while/body/eval_jaxpr/add | solution.py:35
  126.6 3.6 %fusion.65 = bf16[16,8,48,128]{3,2,1,0:T(8,128)(2,1)S(1)} fusion(f32[18,10,50,128]{3,2,1,0:T(8,128)S(1)} %get-tuple-element.161, f32[16,8,50,128]{3,2,1,0:T(8,128)S(1)} %fusion.61, f32[16,8,50,128]{3,2,1,0:T(8,128)S(1)} %fusion.62, f32[18,10,50,128]{3,2,1,0:T(8,128)S(1)} %dynamic-slice_convert_fusion.2, f32[16,8,48]{2,1,0:T(8,128)S(1)} %get-tuple-element.163, ...), kind=kLoop, calls=%fused_computation.40.clone.1 | loop fusion | flops 14155776 | bytes 26787840 | tf_op jit(solution)/shard_map/while/body/eval_jaxpr/convert_element_type | solution.py:64
  130.2 1.9 constant_dynamic-update-slice_fusion.9
  133.3 5.8 %broadcast_multiply_fusion.3 = (f32[18,10,50,128]{3,2,1,0:T(8,128)S(1)}, f32[18,10,50,128]{3,2,1,0:T(8,128)S(1)}) fusion(f32[18,10,50]{2,1,0:T(8,128)S(1)} %get-tuple-element.157, bf16[18,10,50,512]{3,2,1,0:T(8,128)(2,1)} %get-tuple-element.195, s32[]{:T(128)S(6)} %select_n.5, f32[18,10,50]{2,1,0:T(8,128)S(1)} %get-tuple-element.158), kind=kLoop, calls=%fused_computation.52.clone.1 | loop fusion | flops 3456000 | bytes 11592004 | tf_op jit(solution)/shard_map/while/body/eval_jaxpr/mul | solution.py:47
  140.3 2.1 dynamic-slice_convert_fusion.2
  142.3 2.8 multiply_add_fusion.3
  145.8 3.1 fusion.59
  149.8 5.1 %fusion.62 = f32[16,8,50,128]{3,2,1,0:T(8,128)S(1)} fusion(f32[16,10,50,128]{3,2,1,0:T(8,128)} %get-tuple-element.162), kind=kLoop, calls=%fused_computation.22.clone.1 | loop fusion | flops 2457600 | bytes 13107200 | tf_op jit(solution)/shard_map/while/body/eval_jaxpr/add | solution.py:35
  155.2 3.6 %fusion.65 = bf16[16,8,48,128]{3,2,1,0:T(8,128)(2,1)S(1)} fusion(f32[18,10,50,128]{3,2,1,0:T(8,128)S(1)} %get-tuple-element.161, f32[16,8,50,128]{3,2,1,0:T(8,128)S(1)} %fusion.61, f32[16,8,50,128]{3,2,1,0:T(8,128)S(1)} %fusion.62, f32[18,10,50,128]{3,2,1,0:T(8,128)S(1)} %dynamic-slice_convert_fusion.2, f32[16,8,48]{2,1,0:T(8,128)S(1)} %get-tuple-element.163, ...), kind=kLoop, calls=%fused_computation.40.clone.1 | loop fusion | flops 14155776 | bytes 26787840 | tf_op jit(solution)/shard_map/while/body/eval_jaxpr/convert_element_type | solution.py:64
  158.8 1.9 constant_dynamic-update-slice_fusion.9
  162.0 5.8 %broadcast_multiply_fusion.3 = (f32[18,10,50,128]{3,2,1,0:T(8,128)S(1)}, f32[18,10,50,128]{3,2,1,0:T(8,128)S(1)}) fusion(f32[18,10,50]{2,1,0:T(8,128)S(1)} %get-tuple-element.157, bf16[18,10,50,512]{3,2,1,0:T(8,128)(2,1)} %get-tuple-element.195, s32[]{:T(128)S(6)} %select_n.5, f32[18,10,50]{2,1,0:T(8,128)S(1)} %get-tuple-element.158), kind=kLoop, calls=%fused_computation.52.clone.1 | loop fusion | flops 3456000 | bytes 11592004 | tf_op jit(solution)/shard_map/while/body/eval_jaxpr/mul | solution.py:47
  168.9 2.1 dynamic-slice_convert_fusion.2
  171.0 2.8 multiply_add_fusion.3
  174.4 3.1 fusion.59
  178.5 5.1 %fusion.62 = f32[16,8,50,128]{3,2,1,0:T(8,128)S(1)} fusion(f32[16,10,50,128]{3,2,1,0:T(8,128)} %get-tuple-element.162), kind=kLoop, calls=%fused_computation.22.clone.1 | loop fusion | flops 2457600 | bytes 13107200 | tf_op jit(solution)/shard_map/while/body/eval_jaxpr/add | solution.py:35
  183.8 3.6 %fusion.65 = bf16[16,8,48,128]{3,2,1,0:T(8,128)(2,1)S(1)} fusion(f32[18,10,50,128]{3,2,1,0:T(8,128)S(1)} %get-tuple-element.161, f32[16,8,50,128]{3,2,1,0:T(8,128)S(1)} %fusion.61, f32[16,8,50,128]{3,2,1,0:T(8,128)S(1)} %fusion.62, f32[18,10,50,128]{3,2,1,0:T(8,128)S(1)} %dynamic-slice_convert_fusion.2, f32[16,8,48]{2,1,0:T(8,128)S(1)} %get-tuple-element.163, ...), kind=kLoop, calls=%fused_computation.40.clone.1 | loop fusion | flops 14155776 | bytes 26787840 | tf_op jit(solution)/shard_map/while/body/eval_jaxpr/convert_element_type | solution.py:64
  187.4 1.9 constant_dynamic-update-slice_fusion.9
  190.5 5.8 %broadcast_multiply_fusion.3 = (f32[18,10,50,128]{3,2,1,0:T(8,128)S(1)}, f32[18,10,50,128]{3,2,1,0:T(8,128)S(1)}) fusion(f32[18,10,50]{2,1,0:T(8,128)S(1)} %get-tuple-element.157, bf16[18,10,50,512]{3,2,1,0:T(8,128)(2,1)} %get-tuple-element.195, s32[]{:T(128)S(6)} %select_n.5, f32[18,10,50]{2,1,0:T(8,128)S(1)} %get-tuple-element.158), kind=kLoop, calls=%fused_computation.52.clone.1 | loop fusion | flops 3456000 | bytes 11592004 | tf_op jit(solution)/shard_map/while/body/eval_jaxpr/mul | solution.py:47
  197.4 2.1 dynamic-slice_convert_fusion.2
  199.5 2.8 multiply_add_fusion.3
  203.0 3.1 fusion.59
  207.0 5.1 %fusion.62 = f32[16,8,50,128]{3,2,1,0:T(8,128)S(1)} fusion(f32[16,10,50,128]{3,2,1,0:T(8,128)} %get-tuple-element.162), kind=kLoop, calls=%fused_computation.22.clone.1 | loop fusion | flops 2457600 | bytes 13107200 | tf_op jit(solution)/shard_map/while/body/eval_jaxpr/add | solution.py:35
  212.4 3.6 %fusion.65 = bf16[16,8,48,128]{3,2,1,0:T(8,128)(2,1)S(1)} fusion(f32[18,10,50,128]{3,2,1,0:T(8,128)S(1)} %get-tuple-element.161, f32[16,8,50,128]{3,2,1,0:T(8,128)S(1)} %fusion.61, f32[16,8,50,128]{3,2,1,0:T(8,128)S(1)} %fusion.62, f32[18,10,50,128]{3,2,1,0:T(8,128)S(1)} %dynamic-slice_convert_fusion.2, f32[16,8,48]{2,1,0:T(8,128)S(1)} %get-tuple-element.163, ...), kind=kLoop, calls=%fused_computation.40.clone.1 | loop fusion | flops 14155776 | bytes 26787840 | tf_op jit(solution)/shard_map/while/body/eval_jaxpr/convert_element_type | solution.py:64
  215.9 1.8 constant_dynamic-update-slice_fusion.9
  217.8 7.5 %fusion.41 = f32[4,128,512]{2,1,0:T(8,128)S(1)} fusion(bf16[4,6144,128]{2,1,0:T(8,128)(2,1)} %get-tuple-element.65, bf16[6144,512,1]{1,0,2:T(8,128)(2,1)} %bitcast.36), kind=kOutput, calls=%fused_computation.95 | convolution fusion | flops 3221225472 | bytes 13631488 | tf_op jit(solution)/shard_map/cp,bcq->pbq/dot_general | solution.py:89
  225.6 7.5 %fusion.40 = f32[4,128,512]{2,1,0:T(8,128)S(1)} fusion(bf16[4,6144,128]{2,1,0:T(8,128)(2,1)} %get-tuple-element.64, bf16[6144,512,1]{1,0,2:T(8,128)(2,1)} %bitcast.37), kind=kOutput, calls=%fused_computation.94 | convolution fusion | flops 3221225472 | bytes 13631488 | tf_op jit(solution)/shard_map/cp,bcq->pbq/dot_general | solution.py:86
  235.1 44.0 %reduce-scatter.4.cloned.1.call-done = f32[128,1024]{1,0:T(8,128)} async-done(((f32[512,1024]{1,0:T(8,128)}), f32[128,1024]{1,0:T(8,128)}) %reduce-scatter.4.cloned.1.call-update) | async-done | bytes 524304 | tf_op jit(solution)/shard_map/reduce_scatter | solution.py:92
  279.2 27.1 %reduce-scatter.6.cloned.1.call-done = f32[32,1024]{1,0:T(8,128)} async-done(((f32[128,1024]{1,0:T(8,128)}), f32[32,1024]{1,0:T(8,128)}) %reduce-scatter.6.cloned.1.call-update) | async-done | bytes 131088 | tf_op jit(solution)/shard_map/reduce_scatter | solution.py:95
  306.3 9.8 %reduce-scatter.8.cloned.1.call-done = f32[16,1024]{1,0:T(8,128)} async-done(((f32[32,1024]{1,0:T(8,128)}), f32[16,1024]{1,0:T(8,128)}) %reduce-scatter.8.cloned.1.call-update) | async-done | bytes 65552 | tf_op jit(solution)/shard_map/reduce_scatter | solution.py:96
  (102 shorter events, 31.4 us)
Async XLA Ops:
  7.2 272.0 %reduce-scatter.4.cloned.1.call-start = ((), (), s32[]{:S(2)}) async-start(), calls=%async_computation.3 | async-start | bytes 2621440 | tf_op jit(solution)/shard_map/reduce_scatter | solution.py:92
  8.4 13.5 %collective-permute-start.6 = (bf16[1,8,48,512]{3,2,1,0:T(8,128)(2,1)S(1)}, bf16[1,8,48,512]{3,2,1,0:T(8,128)(2,1)S(1)}, u32[]{:S(2)}, u32[]{:S(2)}) collective-permute-start(bf16[1,8,48,512]{3,2,1,0:T(8,128)(2,1)S(1)} %get-tuple-element.95), channel_id=1, source_target_pairs={{0,8},{8,16},{16,24},{1,9},{9,17},{17,25},{2,10},{10,18},{18,26},{... | collective-permute-start | bytes 1179656 | tf_op jit(solution)/shard_map/ppermute | solution.py:20
  14.1 7.8 %collective-permute-start = (f32[2,1,8,48]{3,2,1,0:T(8,128)S(1)}, f32[2,1,8,48]{3,2,1,0:T(8,128)S(1)}, u32[]{:S(2)}, u32[]{:S(2)}) collective-permute-start(f32[2,1,8,48]{3,2,1,0:T(8,128)S(1)} %get-tuple-element.101), channel_id=1, source_target_pairs={{0,8},{8,16},{16,24},{1,9},{9,17},{17,25},{2,10},{10,18},{18,26},{... | collective-permute-start | bytes 9224 | tf_op jit(solution)/shard_map/ppermute | solution.py:20
  17.5 25.3 %collective-permute-start.1 = (f32[2,1,8,48]{3,2,1,0:T(8,128)S(1)}, f32[2,1,8,48]{3,2,1,0:T(8,128)S(1)}, u32[]{:S(2)}, u32[]{:S(2)}) collective-permute-start(f32[2,1,8,48]{3,2,1,0:T(8,128)S(1)} %get-tuple-element.100), channel_id=1, source_target_pairs={{8,0},{16,8},{24,16},{9,1},{17,9},{25,17},{10,2},{18,10},{26,18},{... | collective-permute-start | bytes 9224 | tf_op jit(solution)/shard_map/ppermute | solution.py:22
  18.8 12.8 %collective-permute-start.7 = (bf16[1,8,48,512]{3,2,1,0:T(8,128)(2,1)S(1)}, bf16[1,8,48,512]{3,2,1,0:T(8,128)(2,1)S(1)}, u32[]{:S(2)}, u32[]{:S(2)}) collective-permute-start(bf16[1,8,48,512]{3,2,1,0:T(8,128)(2,1)S(1)} %get-tuple-element.94), channel_id=1, source_target_pairs={{8,0},{16,8},{24,16},{9,1},{17,9},{25,17},{10,2},{18,10},{26,18},{... | collective-permute-start | bytes 1179656 | tf_op jit(solution)/shard_map/ppermute | solution.py:22
  21.9 20.9 %copy-start.3 = (f32[2,16,8,48]{3,2,1,0:T(8,128)S(1)}, f32[2,16,8,48]{3,2,1,0:T(8,128)}, u32[]{:S(2)}) copy-start(f32[2,16,8,48]{3,2,1,0:T(8,128)} %param.5) | copy-start | bytes 147460
  31.7 2.9 copy-start.1
  36.0 49.8 %collective-permute-start.9 = (bf16[18,1,48,512]{3,2,1,0:T(8,128)(2,1)}, bf16[18,1,48,512]{3,2,1,0:T(8,128)(2,1)}, u32[]{:S(2)}, u32[]{:S(2)}) collective-permute-start(bf16[18,1,48,512]{3,2,1,0:T(8,128)(2,1)} %get-tuple-element.93), channel_id=1, source_target_pairs={{2,0},{4,2},{6,4},{3,1},{5,3},{7,5},{10,8},{12,10},{14,12},{11,9},... | collective-permute-start | bytes 2654216 | tf_op jit(solution)/shard_map/ppermute | solution.py:22
  37.3 48.6 %collective-permute-start.8 = (bf16[18,1,48,512]{3,2,1,0:T(8,128)(2,1)}, bf16[18,1,48,512]{3,2,1,0:T(8,128)(2,1)}, u32[]{:S(2)}, u32[]{:S(2)}) collective-permute-start(bf16[18,1,48,512]{3,2,1,0:T(8,128)(2,1)} %get-tuple-element.92), channel_id=1, source_target_pairs={{0,2},{2,4},{4,6},{1,3},{3,5},{5,7},{8,10},{10,12},{12,14},{9,11},... | collective-permute-start | bytes 2654216 | tf_op jit(solution)/shard_map/ppermute | solution.py:20
  42.8 51.3 %slice-start = ((s8[7077888]{0:T(1024)(128)(4,1)}), s8[2883584]{0:T(1024)(128)(4,1)S(1)}, s32[]{:S(2)}) async-start(s8[7077888]{0:T(1024)(128)(4,1)} %bitcast.38), calls=%async_computation.6 | async-start | bytes 5767168
  42.9 34.7 %collective-permute-start.3 = (f32[2,18,1,48]{3,2,1,0:T(1,128)S(1)}, f32[2,18,1,48]{3,2,1,0:T(1,128)S(1)}, u32[]{:S(2)}, u32[]{:S(2)}) collective-permute-start(f32[2,18,1,48]{3,2,1,0:T(1,128)S(1)} %get-tuple-element.99), channel_id=1, source_target_pairs={{2,0},{4,2},{6,4},{3,1},{5,3},{7,5},{10,8},{12,10},{14,12},{11,9},... | collective-permute-start | bytes 20744 | tf_op jit(solution)/shard_map/ppermute | solution.py:22
  44.4 33.2 %collective-permute-start.2 = (f32[2,18,1,48]{3,2,1,0:T(1,128)S(1)}, f32[2,18,1,48]{3,2,1,0:T(1,128)S(1)}, u32[]{:S(2)}, u32[]{:S(2)}) collective-permute-start(f32[2,18,1,48]{3,2,1,0:T(1,128)S(1)} %get-tuple-element.98), channel_id=1, source_target_pairs={{0,2},{2,4},{4,6},{1,3},{3,5},{5,7},{8,10},{10,12},{12,14},{9,11},... | collective-permute-start | bytes 20744 | tf_op jit(solution)/shard_map/ppermute | solution.py:20
  78.6 5.1 %collective-permute-start.5 = (f32[2,18,10,1]{3,2,1,0:T(8,128)}, f32[2,18,10,1]{3,2,1,0:T(8,128)S(1)}, u32[]{:S(2)}, u32[]{:S(2)}) collective-permute-start(f32[2,18,10,1]{3,2,1,0:T(8,128)} %get-tuple-element.97), channel_id=1, source_target_pairs={{1,0},{3,2},{5,4},{7,6},{9,8},{11,10},{13,12},{15,14},{17,16},{19,... | collective-permute-start | bytes 4328 | tf_op jit(solution)/shard_map/ppermute | solution.py:22
  79.9 4.6 %collective-permute-start.4 = (f32[2,18,10,1]{3,2,1,0:T(8,128)}, f32[2,18,10,1]{3,2,1,0:T(8,128)}, u32[]{:S(2)}, u32[]{:S(2)}) collective-permute-start(f32[2,18,10,1]{3,2,1,0:T(8,128)} %get-tuple-element.96), channel_id=1, source_target_pairs={{0,1},{2,3},{4,5},{6,7},{8,9},{10,11},{12,13},{14,15},{16,17},{18,... | collective-permute-start | bytes 4328 | tf_op jit(solution)/shard_map/ppermute | solution.py:20
  83.7 0.7 copy-start.2
  85.8 8.3 %slice-start.1 = ((s8[7077888]{0:T(1024)(128)(4,1)}), s8[4194304]{0:T(1024)(128)(4,1)S(1)}, s32[]{:S(2)}) async-start(s8[7077888]{0:T(1024)(128)(4,1)} %bitcast.38), calls=%async_computation.7 | async-start | bytes 8388608
  88.4 4.6 %collective-permute-start.11 = (bf16[18,10,1,512]{3,2,1,0:T(2,128)(2,1)S(1)}, bf16[18,10,1,512]{3,2,1,0:T(2,128)(2,1)S(1)}, u32[]{:S(2)}, u32[]{:S(2)}) collective-permute-start(bf16[18,10,1,512]{3,2,1,0:T(2,128)(2,1)S(1)} %get-tuple-element.91), channel_id=1, source_target_pairs={{1,0},{3,2},{5,4},{7,6},{9,8},{11,10},{13,12},{15,14},{17,16},{19,... | collective-permute-start | bytes 552968 | tf_op jit(solution)/shard_map/ppermute | solution.py:22
  89.7 4.4 %collective-permute-start.10 = (bf16[18,10,1,512]{3,2,1,0:T(2,128)(2,1)S(1)}, bf16[18,10,1,512]{3,2,1,0:T(2,128)(2,1)S(1)}, u32[]{:S(2)}, u32[]{:S(2)}) collective-permute-start(bf16[18,10,1,512]{3,2,1,0:T(2,128)(2,1)S(1)} %get-tuple-element.90), channel_id=1, source_target_pairs={{0,1},{2,3},{4,5},{6,7},{8,9},{10,11},{12,13},{14,15},{16,17},{18,... | collective-permute-start | bytes 552968 | tf_op jit(solution)/shard_map/ppermute | solution.py:20
  126.6 3.6 %copy-start = (bf16[16,8,48,128]{3,2,1,0:T(8,128)(2,1)S(1)}, bf16[16,8,48,128]{3,2,1,0:T(8,128)(2,1)}, u32[]{:S(2)}) copy-start(bf16[16,8,48,128]{3,2,1,0:T(8,128)(2,1)} %fusion.59) | copy-start | bytes 4718596 | tf_op jit(solution)/shard_map/while
  155.2 3.6 %copy-start = (bf16[16,8,48,128]{3,2,1,0:T(8,128)(2,1)S(1)}, bf16[16,8,48,128]{3,2,1,0:T(8,128)(2,1)}, u32[]{:S(2)}) copy-start(bf16[16,8,48,128]{3,2,1,0:T(8,128)(2,1)} %fusion.59) | copy-start | bytes 4718596 | tf_op jit(solution)/shard_map/while
  183.8 3.6 %copy-start = (bf16[16,8,48,128]{3,2,1,0:T(8,128)(2,1)S(1)}, bf16[16,8,48,128]{3,2,1,0:T(8,128)(2,1)}, u32[]{:S(2)}) copy-start(bf16[16,8,48,128]{3,2,1,0:T(8,128)(2,1)} %fusion.59) | copy-start | bytes 4718596 | tf_op jit(solution)/shard_map/while
  212.3 3.6 %copy-start = (bf16[16,8,48,128]{3,2,1,0:T(8,128)(2,1)S(1)}, bf16[16,8,48,128]{3,2,1,0:T(8,128)(2,1)}, u32[]{:S(2)}) copy-start(bf16[16,8,48,128]{3,2,1,0:T(8,128)(2,1)} %fusion.59) | copy-start | bytes 4718596 | tf_op jit(solution)/shard_map/while
  235.1 71.2 %reduce-scatter.6.cloned.1.call-start = ((), (), s32[]{:S(2)}) async-start(), calls=%async_computation.4 | async-start | bytes 655360 | tf_op jit(solution)/shard_map/reduce_scatter | solution.py:95
  279.2 36.9 %reduce-scatter.8.cloned.1.call-start = ((), (), s32[]{:S(2)}) async-start(), calls=%async_computation.5 | async-start | bytes 196608 | tf_op jit(solution)/shard_map/reduce_scatter | solution.py:96
Sparse Core Ops, SparseCore 0:
  235.2 43.9 reduce-scatter.3
  282.0 24.2 reduce-scatter.5
  308.5 7.5 reduce-scatter.7
where the time goes:
time: 325 us; the launch traced here: 324 us
  waiting for transfers between devices  118 us (36%)
  other arithmetic  118 us (36%)
  starting transfers between devices  33.6 us (10%)
  local copies, waits for them, and re-layouts  22.4 us (7%)
  matrix products  15 us (5%)
  between operations  14 us (4%)
    reduce_scatter x1, waiting for transfers between devices, per_device(): lax.psum_scatter(jnp.concatenate([stiff_part, mass_part], axis=1), 'gx',...  44 us
    add x37, other arithmetic, three_taps(): field = side * (lower + upper) + middle * centre  42.2 us
    ppermute x6, waiting for transfers between devices, with_halo(): lax.ppermute(head, axis, [((i + 1) % count, i) for i in range(ends)])  34.5 us
    reduce_scatter x1, waiting for transfers between devices, per_device(): lax.psum_scatter(section_one, 'gy', scatter_dimension=0, tiled=True)  27.1 us
    convert_element_type x8, other arithmetic, apply_operators(): return (stiff_sum.astype(jnp.bfloat16), mass_sum.astype(jnp.bfloat16))  26.8 us
    ppermute x6, starting transfers between devices, with_halo(): lax.ppermute(tail, axis, [(i, (i + 1) % count) for i in range(ends)])  25.5 us
    mul x4, other arithmetic, apply_operators(): rho_values = rho[..., None] * values  23.2 us
    concatenate x3, other arithmetic, with_halo(): jnp.concatenate([lax.ppermute(tail, axis, [(i, (i + 1) % count) for i in...  10.8 us
  transfers between devices with their start and end apart: 15, of which 8 were waited for; matrix products, arithmetic and copies ran while one was open for 3% of the time, Pallas kernels for 0%

commit v1 on v0

v1 whole, which is shorter than its diff:
```python
import functools
import numpy as np
import jax
import jax.numpy as jnp
from jax import lax
from jax.experimental import pallas as pl
from jax.experimental.pallas import tpu as pltpu
from jax.sharding import PartitionSpec as P


def upper(cells, axis, dim):
    count = lax.axis_size(axis)
    head = lax.slice_in_dim(cells, 0, 1, axis=dim)
    return lax.ppermute(head, axis, [(i + 1, i) for i in range(count - 1)])


def taps(count, middle):
    t = middle * np.eye(count) + np.eye(count, k=1) + np.eye(count, k=-1)
    t[-1, -1] = 0.0
    return t


def rows_of(size_y, size_z):
    order = np.zeros((size_y + 1, size_z + 1), np.int64)
    for y in range(size_y + 1):
        order[y, :size_z] = y * size_z + np.arange(size_z)
        order[y, size_z] = (size_y + 1) * size_z + y
    return order


def plane_matrix(size_y, size_z, rows):
    order = rows_of(size_y, size_z).reshape(-1)
    blocks = []
    for middle in (2.0, 4.0):
        full = np.kron(taps(size_y + 1, middle), taps(size_z + 1, middle))
        block = np.zeros((rows, rows))
        block[np.ix_(order, order)] = full
        blocks.append(block)
    return np.concatenate(blocks, 0)


def coefficients(ext, rows, cells_shape):
    size_x, size_y, size_z = cells_shape
    kappa, rho = ext[0], ext[1]
    field = kappa
    for dim in range(3):
        n = field.shape[dim]
        pad = [(1, 1) if d == dim else (0, 0) for d in range(3)]
        wide = jnp.pad(field, pad)
        lower = lax.slice_in_dim(wide, 0, n, axis=dim)
        above = lax.slice_in_dim(wide, 2, n + 2, axis=dim)
        shape = [1, 1, 1]
        shape[dim] = n
        diag = jnp.asarray(np.r_[np.full(n - 1, 2.0), 0.0].reshape(shape), jnp.float32)
        field = lower + above + diag * field
    owned = np.zeros(kappa.shape, np.float32)
    owned[:size_x, :size_y, :size_z] = 2.0
    diag = owned * kappa + field * (1.0 / 32.0)
    parts = jnp.stack([diag, kappa * (1.0 / 16.0), rho * (1.0 / 216.0)], axis=1)
    main = parts[..., :size_z].reshape(size_x + 1, 3, (size_y + 1) * size_z)
    edge = parts[..., size_z]
    both = jnp.concatenate([main, edge], axis=2)
    return jnp.pad(both, ((0, 0), (0, 5), (0, rows - both.shape[2])))


def kernel(scale, e_ref, t_ref, c_ref, out_ref, pq, acc):
    planes, rows, columns = e_ref.shape

    def taps_of(x):
        pq[lax.rem(x, 3)] = jnp.dot(t_ref[...], e_ref[x], preferred_element_type=jnp.float32)

    acc[...] = jnp.zeros_like(acc)
    pq[2] = jnp.zeros(pq.shape[1:], jnp.float32)
    taps_of(0)

    def step(x, carry):
        now, after, before = lax.rem(x, 3), lax.rem(x + 1, 3), lax.rem(x + 2, 3)

        @pl.when(x < planes - 1)
        def _():
            taps_of(x + 1)

        @pl.when(x == planes - 1)
        def _():
            pq[after] = jnp.zeros(pq.shape[1:], jnp.float32)

        last = x == planes - 1
        two = jnp.where(last, 0.0, 2.0)
        four = jnp.where(last, 0.0, 4.0)
        coef = c_ref[x].T
        v = e_ref[x]
        stiff = pq[before, :rows] + pq[after, :rows] + two * pq[now, :rows]
        yk = coef[:, 0:1] * v.astype(jnp.float32) - coef[:, 1:2] * stiff
        mass = pq[before, rows:] + pq[after, rows:] + four * pq[now, rows:]
        ym = coef[:, 2:3] * mass
        dims = (((0,), (0,)), ((), ()))
        acc[:, :columns] += lax.dot_general(v, yk.astype(jnp.bfloat16), dims, preferred_element_type=jnp.float32)
        acc[:, columns:] += lax.dot_general(v, ym.astype(jnp.bfloat16), dims, preferred_element_type=jnp.float32)
        return carry

    lax.fori_loop(0, planes, step, 0)
    for half in range(2):
        m = acc[:, half * columns:(half + 1) * columns]
        out_ref[:, half * columns:(half + 1) * columns] = (m + m.T) * scale


def per_device(eigvecs, material):
    size_x, size_y, size_z, columns = eigvecs.shape
    axes = ("gx", "gy", "gz")
    devices_all = 1
    for axis in axes:
        devices_all *= lax.axis_size(axis)
    total_cells = size_x * size_y * size_z * devices_all
    ext = material
    for axis, dim in (("gz", 3), ("gy", 2), ("gx", 1)):
        ext = jnp.concatenate([ext, upper(ext, axis, dim)], axis=dim)
    rows = -(-((size_y + 1) * (size_z + 1)) // 16) * 16
    coef = coefficients(ext, rows, (size_x, size_y, size_z))
    z_edge = upper(eigvecs, "gz", 2)[:, :, 0]
    y_face = upper(eigvecs, "gy", 1)[:, 0]
    y_edge = upper(z_edge, "gy", 1)
    tail = rows - (size_y + 1) * (size_z + 1)
    plane = jnp.concatenate(
        [eigvecs.reshape(size_x, size_y * size_z, columns), y_face, z_edge, y_edge,
         jnp.zeros((size_x, tail, columns), eigvecs.dtype)], axis=1)
    extended = jnp.concatenate([plane, upper(plane, "gx", 0)], axis=0)
    matrix = jnp.asarray(plane_matrix(size_y, size_z, rows), jnp.bfloat16)
    part = pl.pallas_call(
        functools.partial(kernel, 0.5 / total_cells),
        out_shape=jax.ShapeDtypeStruct((columns, 2 * columns), jnp.float32),
        in_specs=[pl.BlockSpec(memory_space=pltpu.VMEM)] * 3,
        out_specs=pl.BlockSpec(memory_space=pltpu.VMEM),
        scratch_shapes=[
            pltpu.VMEM((3, 2 * rows, columns), jnp.float32),
            pltpu.VMEM((columns, 2 * columns), jnp.float32),
        ],
        compiler_params=pltpu.CompilerParams(vmem_limit_bytes=60 * 1024 * 1024),
    )(extended, matrix, coef)
    summed = part
    for axis in axes:
        summed = lax.psum_scatter(summed, axis, scatter_dimension=0, tiled=True)
    return (summed[:, :columns], summed[:, columns:])


def solution(mesh):
    return jax.shard_map(
        per_device,
        mesh=mesh,
        in_specs=(P("gx", "gy", "gz", None), P(None, "gx", "gy", "gz")),
        out_specs=(P(("gx", "gy", "gz"), None), P(("gx", "gy", "gz"), None)),
        check_vma=False,
    )
```

time: 325 us -> 221 us (0.68)
  other arithmetic: 118 us -> 11.1 us
  Pallas kernels: 0 us -> 36.3 us
  starting transfers between devices: 33.6 us -> 9.14 us
  local copies, waits for them, and re-layouts: 22.4 us -> 40.1 us
  matrix products: 15 us -> 0 us
  waiting for transfers between devices: 118 us -> 109 us
    add x37 -> x2, other arithmetic: 42.2 us -> 1.48 us  [coefficients(): field = lower + above + diag * field]
    pallas_call x0 -> x1, Pallas kernels: none -> 36.3 us  [per_device(): pl.pallas_call(functools.partial(kernel, 0.5 / total_cells), out_shape=ja...]
    convert_element_type x12 -> x0, other arithmetic: 35.1 us -> none  [the longest x8 26.8 us: apply_operators(): return (stiff_sum.astype(jnp.bfloat16), mass_sum.astype(jnp.bfloat16))]
    concatenate x2 -> x1, local copies, waits for them, and re-layouts: 0.03 us -> 29.8 us  [per_device(): jnp.concatenate([eigvecs.reshape(size_x, size_y * size_z, columns), y_fac...]
    ppermute x12 -> x7, starting transfers between devices: 33.5 us -> 9.02 us  [upper(): return lax.ppermute(head, axis, [(i + 1, i) for i in range(count - 1)])]
    mul x12 -> x0, other arithmetic: 24 us -> none  [the longest x4 23.2 us: apply_operators(): rho_values = rho[..., None] * values]
    dot_general x2 -> x0, matrix products: 15 us -> none  [the longest x1 7.52 us: per_device(): jnp.einsum('cp,bcq->pbq', flat_vectors, stiff_blocks, preferred_element_t...]
    ppermute x12 -> x7, waiting for transfers between devices: 37.4 us -> 28.5 us  [upper(): return lax.ppermute(head, axis, [(i + 1, i) for i in range(count - 1)])]
  transfers between devices with their start and end apart: 15 -> 10, of which waited for: 8 -> 8; matrix products, arithmetic and copies ran while one was open for 3% -> 5% of each run, Pallas kernels for 0% -> 0%
where the time goes in v1:
time: 221 us; the launch traced here: 220 us
  waiting for transfers between devices  109 us (49%)
  local copies, waits for them, and re-layouts  40.1 us (18%)
  Pallas kernels  36.3 us (16%)
  between operations  14 us (6%)
  other arithmetic  11.1 us (5%)
  starting transfers between devices  9.14 us (4%)
    reduce_scatter x3, waiting for transfers between devices, per_device(): summed = lax.psum_scatter(summed, axis, scatter_dimension=0, tiled=True)  80.9 us
    pallas_call x1, Pallas kernels, per_device(): pl.pallas_call(functools.partial(kernel, 0.5 / total_cells), out_shape=ja...  36.3 us
    concatenate x1, local copies, waits for them, and re-layouts, per_device(): jnp.concatenate([eigvecs.reshape(size_x, size_y * size_z, columns), y_fac...  29.8 us
    ppermute x7, waiting for transfers between devices, upper(): return lax.ppermute(head, axis, [(i + 1, i) for i in range(count - 1)])  28.5 us
    ppermute x7, starting transfers between devices, upper(): return lax.ppermute(head, axis, [(i + 1, i) for i in range(count - 1)])  9.02 us
    concatenate x1, other arithmetic, per_device(): extended = jnp.concatenate([plane, upper(plane, 'gx', 0)], axis=0)  6.96 us
  transfers between devices with their start and end apart: 10, of which 8 were waited for; matrix products, arithmetic and copies ran while one was open for 5% of the time, Pallas kernels for 0%

profile of v1, /device:TPU:0, one launch (start us, length us, event | category | flops | bytes accessed | tf_op | source)
XLA Modules:
  0.0 220.1 jit_solution(11115422818525724844)
XLA Ops:
  7.2 0.0 reduce-scatter.4.cloned.1.call-start
  7.2 0.9 copy.58
  8.1 1.3 collective-permute-start.4
  9.4 1.9 collective-permute-done.4
  11.4 0.1 pad_maximum_fusion.3
  11.5 1.3 collective-permute-start.5
  12.8 5.3 %collective-permute-done.5 = f32[2,16,1,49]{3,1,2,0:T(8,128)S(1)} collective-permute-done((f32[2,16,1,49]{3,1,2,0:T(8,128)S(1)}, f32[2,16,1,49]{3,1,2,0:T(8,128)S(1)}, u32[]{:S(2)}, u32[]{:S(2)}) %collective-permute-start.5) | collective-permute-done | bytes 6304 | tf_op jit(solution)/shard_map/ppermute | solution.py:14
  18.0 0.1 pad_maximum_fusion.4
  18.1 1.3 collective-permute-start.6
  19.4 1.2 slice_bitcast_fusion
  20.6 1.3 collective-permute-start
  21.9 1.4 slice.58
  23.4 1.3 collective-permute-start.1
  24.7 0.0 collective-permute-done.6
  24.7 0.1 pad_maximum_fusion.2
  24.8 0.7 multiply_add_fusion
  25.6 1.1 collective-permute-done.1
  26.6 1.3 collective-permute-start.2
  27.9 0.7 fusion.1
  28.7 14.2 %collective-permute-done.2 = bf16[16,1,512]{2,1,0:T(2,128)(2,1)S(1)} collective-permute-done((bf16[16,1,512]{2,1,0:T(2,128)(2,1)S(1)}, bf16[16,1,512]{2,1,0:T(2,128)(2,1)S(1)}, u32[]{:S(2)}, u32[]{:S(2)}) %collective-permute-start.2) | collective-permute-done | bytes 16416 | tf_op jit(solution)/shard_map/ppermute | solution.py:14
  42.8 0.0 collective-permute-done
  42.9 0.0 copy-start
  42.9 0.0 copy-start.1
  42.9 29.8 %concatenate.18 = bf16[16,448,512]{2,1,0:T(8,128)(2,1)} concatenate(bf16[16,384,512]{2,1,0:T(8,128)(2,1)} %bitcast.18, bf16[16,48,512]{2,1,0:T(8,128)(2,1)S(1)} %bitcast.20, bf16[16,8,512]{2,1,0:T(8,128)(2,1)S(1)} %bitcast.22, bf16[16,1,512]{2,1,0:T(2,128)(2,1)S(1)} %collective-permute-done.2, bf16[16,7,512]{2,1,0:T(8,128)(2,1)S(1)} %broadcast_in_dim.3), dimensions={1} | concatenate | bytes 14680064 | tf_op jit(solution)/shard_map/concatenate | solution.py:123
  72.7 1.8 slice.77
  74.5 1.3 collective-permute-start.3
  75.8 0.0 copy-done
  75.8 0.1 add_bitcast_fusion
  75.9 0.6 copy.63
  76.6 0.6 copy.62
  77.2 0.6 copy.61
  77.8 1.5 pad_maximum_fusion.1
  79.3 0.3 slice.81
  79.6 1.2 copy.70
  80.8 0.2 reshape.36
  81.0 0.8 select_maximum_fusion.c_ref
  81.8 6.1 %collective-permute-done.3 = bf16[1,448,512]{2,1,0:T(8,128)(2,1)} collective-permute-done((bf16[1,448,512]{2,1,0:T(8,128)(2,1)}, bf16[1,448,512]{2,1,0:T(8,128)(2,1)}, u32[]{:S(2)}, u32[]{:S(2)}) %collective-permute-start.3) | collective-permute-done | bytes 458784 | tf_op jit(solution)/shard_map/ppermute | solution.py:14
  87.9 7.0 %pad_maximum_fusion.e_ref = bf16[17,448,512]{2,1,0:T(8,128)(2,1)} fusion(bf16[1,448,512]{2,1,0:T(8,128)(2,1)} %collective-permute-done.3, bf16[16,448,512]{2,1,0:T(8,128)(2,1)} %concatenate.18), kind=kLoop, calls=%fused_computation | loop fusion | flops 3899392 | bytes 15597568 | tf_op jit(solution)/shard_map/concatenate | solution.py:126
  94.8 36.3 %shard_map.86 = f32[512,1024]{1,0:T(8,128)} custom-call(bf16[17,448,512]{2,1,0:T(8,128)(2,1)} %pad_maximum_fusion.e_ref, bf16[896,448]{1,0:T(8,128)(2,1)} %constant.25.clone.t_ref, f32[17,8,448]{2,1,0:T(8,128)} %select_maximum_fusion.c_ref), custom_call_target="tpu_custom_call" | custom-call | tf_op jit(solution)/shard_map/pallas_call | solution.py:128
  131.1 0.0 reduce-scatter.4.cloned.1.call-update
  131.1 0.0 reduce-scatter.6.cloned.1.call-start
  131.2 44.0 %reduce-scatter.4.cloned.1.call-done = f32[128,1024]{1,0:T(8,128)} async-done(((f32[512,1024]{1,0:T(8,128)}), f32[128,1024]{1,0:T(8,128)}) %reduce-scatter.4.cloned.1.call-update) | async-done | bytes 524304 | tf_op jit(solution)/shard_map/reduce_scatter | solution.py:141
  175.2 0.0 reduce-scatter.6.cloned.1.call-update
  175.3 0.0 reduce-scatter.8.cloned.1.call-start
  175.3 27.1 %reduce-scatter.6.cloned.1.call-done = f32[32,1024]{1,0:T(8,128)} async-done(((f32[128,1024]{1,0:T(8,128)}), f32[32,1024]{1,0:T(8,128)}) %reduce-scatter.6.cloned.1.call-update) | async-done | bytes 131088 | tf_op jit(solution)/shard_map/reduce_scatter | solution.py:141
  202.4 0.0 reduce-scatter.8.cloned.1.call-update
  202.4 9.8 %reduce-scatter.8.cloned.1.call-done = f32[16,1024]{1,0:T(8,128)} async-done(((f32[32,1024]{1,0:T(8,128)}), f32[16,1024]{1,0:T(8,128)}) %reduce-scatter.8.cloned.1.call-update) | async-done | bytes 65552 | tf_op jit(solution)/shard_map/reduce_scatter | solution.py:141
  212.2 1.4 fusion.3
  (6 shorter events, 0.1 us)
Async XLA Ops:
  7.2 168.1 %reduce-scatter.4.cloned.1.call-start = ((), (), s32[]{:S(2)}) async-start(), calls=%async_computation.3 | async-start | bytes 2621440 | tf_op jit(solution)/shard_map/reduce_scatter | solution.py:141
  8.1 3.2 %collective-permute-start.4 = (f32[2,16,8,1]{3,1,2,0:T(8,128)S(1)}, f32[2,16,8,1]{3,1,2,0:T(8,128)S(1)}, u32[]{:S(2)}, u32[]{:S(2)}) collective-permute-start(f32[2,16,8,1]{3,1,2,0:T(8,128)S(1)} %bitcast.19), channel_id=1, source_target_pairs={{1,0},{3,2},{5,4},{7,6},{9,8},{11,10},{13,12},{15,14},{17,16},{19,... | collective-permute-start | bytes 3080 | tf_op jit(solution)/shard_map/ppermute | solution.py:14
  11.5 6.6 %collective-permute-start.5 = (f32[2,16,1,49]{3,1,2,0:T(8,128)S(1)}, f32[2,16,1,49]{3,1,2,0:T(8,128)S(1)}, u32[]{:S(2)}, u32[]{:S(2)}) collective-permute-start(f32[2,16,1,49]{3,1,2,0:T(8,128)S(1)} %pad_maximum_fusion.3), channel_id=1, source_target_pairs={{2,0},{4,2},{6,4},{3,1},{5,3},{7,5},{10,8},{12,10},{14,12},{11,9},... | collective-permute-start | bytes 18824 | tf_op jit(solution)/shard_map/ppermute | solution.py:14
  18.1 6.5 %collective-permute-start.6 = (f32[2,1,9,49]{3,1,2,0:T(1,128)S(1)}, f32[2,1,9,49]{3,1,2,0:T(1,128)S(1)}, u32[]{:S(2)}, u32[]{:S(2)}) collective-permute-start(f32[2,1,9,49]{3,1,2,0:T(1,128)S(1)} %pad_maximum_fusion.4), channel_id=1, source_target_pairs={{8,0},{16,8},{24,16},{9,1},{17,9},{25,17},{10,2},{18,10},{26,18},{... | collective-permute-start | bytes 10592 | tf_op jit(solution)/shard_map/ppermute | solution.py:14
  20.6 22.2 %collective-permute-start = (bf16[16,1,48,512]{3,2,0,1:T(8,128)(2,1)S(1)}, bf16[16,1,48,512]{3,2,0,1:T(8,128)(2,1)S(1)}, u32[]{:S(2)}, u32[]{:S(2)}) collective-permute-start(bf16[16,1,48,512]{3,2,0,1:T(8,128)(2,1)S(1)} %slice_bitcast_fusion), channel_id=1, source_target_pairs={{2,0},{4,2},{6,4},{3,1},{5,3},{7,5},{10,8},{12,10},{14,12},{11,9},... | collective-permute-start | bytes 2359304 | tf_op jit(solution)/shard_map/ppermute | solution.py:14
  23.4 3.2 %collective-permute-start.1 = (bf16[16,8,1,512]{3,1,0,2:T(8,128)(2,1)S(1)}, bf16[16,8,1,512]{3,1,0,2:T(8,128)(2,1)S(1)}, u32[]{:S(2)}, u32[]{:S(2)}) collective-permute-start(bf16[16,8,1,512]{3,1,0,2:T(8,128)(2,1)S(1)} %copy.73), channel_id=1, source_target_pairs={{1,0},{3,2},{5,4},{7,6},{9,8},{11,10},{13,12},{15,14},{17,16},{19,... | collective-permute-start | bytes 393224 | tf_op jit(solution)/shard_map/ppermute | solution.py:14
  26.6 16.2 %collective-permute-start.2 = (bf16[16,1,512]{2,1,0:T(2,128)(2,1)S(1)}, bf16[16,1,512]{2,1,0:T(2,128)(2,1)S(1)}, u32[]{:S(2)}, u32[]{:S(2)}) collective-permute-start(bf16[16,1,512]{2,1,0:T(2,128)(2,1)S(1)} %slice.76), channel_id=1, source_target_pairs={{2,0},{4,2},{6,4},{3,1},{5,3},{7,5},{10,8},{12,10},{14,12},{11,9},... | collective-permute-start | bytes 49160 | tf_op jit(solution)/shard_map/ppermute | solution.py:14
  42.9 32.9 %copy-start = (f32[17,9,49]{2,0,1:T(8,128)S(1)}, f32[17,9,49]{2,0,1:T(8,128)}, u32[]{:S(2)}) copy-start(f32[17,9,49]{2,0,1:T(8,128)} %constant.24.clone) | copy-start | bytes 89968
  42.9 32.9 %copy-start.1 = (f32[49]{0:T(128)S(1)}, f32[49]{0:T(128)}, u32[]{:S(2)}) copy-start(f32[49]{0:T(128)} %constant.36) | copy-start | bytes 592
  74.5 13.4 %collective-permute-start.3 = (bf16[1,448,512]{2,1,0:T(8,128)(2,1)}, bf16[1,448,512]{2,1,0:T(8,128)(2,1)}, u32[]{:S(2)}, u32[]{:S(2)}) collective-permute-start(bf16[1,448,512]{2,1,0:T(8,128)(2,1)} %slice.77), channel_id=1, source_target_pairs={{8,0},{16,8},{24,16},{9,1},{17,9},{25,17},{10,2},{18,10},{26,18},{... | collective-permute-start | bytes 1376264 | tf_op jit(solution)/shard_map/ppermute | solution.py:14
  131.1 71.2 %reduce-scatter.6.cloned.1.call-start = ((), (), s32[]{:S(2)}) async-start(), calls=%async_computation.4 | async-start | bytes 655360 | tf_op jit(solution)/shard_map/reduce_scatter | solution.py:141
  175.3 37.0 %reduce-scatter.8.cloned.1.call-start = ((), (), s32[]{:S(2)}) async-start(), calls=%async_computation.5 | async-start | bytes 196608 | tf_op jit(solution)/shard_map/reduce_scatter | solution.py:141
Sparse Core Ops, SparseCore 0:
  131.3 43.9 reduce-scatter.3
  178.1 24.2 reduce-scatter.5
  204.6 7.5 reduce-scatter.7

commit v2 on v1

--- a/solution.py
+++ b/solution.py
@@ -102,6 +102,112 @@
     for half in range(2):
         m = acc[:, half * columns:(half + 1) * columns]
         out_ref[:, half * columns:(half + 1) * columns] = (m + m.T) * scale
+
+
+def spread(axis, piece, landing, send, recv):
+    count = lax.axis_size(axis)
+    me = lax.axis_index(axis)
+    copies = []
+    for k in range(1, count):
+        peer = lax.rem(me + k, count)
+        copy = pltpu.make_async_remote_copy(
+            src_ref=piece(peer), dst_ref=landing.at[k - 1],
+            send_sem=send.at[k - 1], recv_sem=recv.at[k - 1],
+            device_id={axis: peer}, device_id_type=pl.DeviceIdType.MESH)
+        copy.start()
+        copies.append(copy)
+    return copies
+
+
+def greet(axes):
+    barrier = pltpu.get_barrier_semaphore()
+    total = 0
+    for axis in axes:
+        count = lax.axis_size(axis)
+        me = lax.axis_index(axis)
+        for k in range(1, count):
+            pl.semaphore_signal(barrier, inc=1, device_id={axis: lax.rem(me + k, count)},
+                                device_id_type=pl.DeviceIdType.MESH)
+        total += count - 1
+    pl.semaphore_wait(barrier, total)
+
+
+def reduce_kernel(cut, part, stiff_out, mass_out, rz, sa, sb, ra1, rb1, ta, tb, ra2, rb2, out,
+                  *sems):
+    z_send, z_recv, a1s, a1r, b1s, b1r, a2s, a2r, b2s, b2r = sems
+    gx, gy, gz = (lax.axis_index(a) for a in ("gx", "gy", "gz"))
+    greet(("gx", "gy", "gz"))
+    first = spread("gz", lambda p: part.at[:, :, p], rz, z_send, z_recv)
+    for copy in first:
+        copy.wait_recv()
+    held = part[:, :, gz]
+    for k in range(len(first)):
+        held = held + rz[k]
+    sa[...] = held[..., :cut]
+    sb[...] = held[..., cut:]
+    a1 = spread("gy", lambda p: sa.at[:, p], ra1, a1s, a1r)
+    b1 = spread("gx", lambda p: sb.at[p], rb1, b1s, b1r)
+    for copy in a1:
+        copy.wait_recv()
+    held = sa[:, gy]
+    for k in range(len(a1)):
+        held = held + ra1[k]
+    ta[...] = held
+    a2 = spread("gx", lambda p: ta.at[p], ra2, a2s, a2r)
+    for copy in b1:
+        copy.wait_recv()
+    held = sb[gx]
+    for k in range(len(b1)):
+        held = held + rb1[k]
+    tb[...] = held
+    b2 = spread("gy", lambda p: tb.at[p], rb2, b2s, b2r)
+    for copy in a2:
+        copy.wait_recv()
+    held = ta[gx]
+    for k in range(len(a2)):
+        held = held + ra2[k]
+    out[:, :cut] = held
+    for copy in b2:
+        copy.wait_recv()
+    held = tb[gy]
+    for k in range(len(b2)):
+        held = held + rb2[k]
+    out[:, cut:] = held
+    columns = stiff_out.shape[1]
+    stiff_out[...] = out[:, :columns]
+    mass_out[...] = out[:, columns:]
+    for copy in first + a1 + b1 + a2 + b2:
+        copy.wait_send()
+
+
+def reduced(part):
+    nx, ny, nz = (lax.axis_size(a) for a in ("gx", "gy", "gz"))
+    wide = part.shape[1]
+    rows = part.shape[0] // (nx * ny * nz)
+    cut = (wide * 5 // 8) // 128 * 128
+    rest = wide - cut
+    f32 = jnp.float32
+    dma = pltpu.SemaphoreType.DMA
+    vmem = pl.BlockSpec(memory_space=pltpu.VMEM)
+    return pl.pallas_call(
+        functools.partial(reduce_kernel, cut),
+        out_shape=[jax.ShapeDtypeStruct((rows, wide // 2), f32)] * 2,
+        in_specs=[vmem],
+        out_specs=[vmem, vmem],
+        scratch_shapes=[
+            pltpu.VMEM((nz - 1, nx, ny, rows, wide), f32),
+            pltpu.VMEM((nx, ny, rows, cut), f32),
+            pltpu.VMEM((nx, ny, rows, rest), f32),
+            pltpu.VMEM((ny - 1, nx, rows, cut), f32),
+            pltpu.VMEM((nx - 1, ny, rows, rest), f32),
+            pltpu.VMEM((nx, rows, cut), f32),
+            pltpu.VMEM((ny, rows, rest), f32),
+            pltpu.VMEM((nx - 1, rows, cut), f32),
+            pltpu.VMEM((ny - 1, rows, rest), f32),
+            pltpu.VMEM((rows, wide), f32),
+        ] + [dma((n - 1,)) for n in (nz, nz, ny, ny, nx, nx, nx, nx, ny, ny)],
+        compiler_params=pltpu.CompilerParams(collective_id=1, has_side_effects=True),
+    )(part.reshape(nx, ny, nz, rows, wide))
 
 
 def per_device(eigvecs, material):
@@ -136,10 +242,7 @@
         ],
         compiler_params=pltpu.CompilerParams(vmem_limit_bytes=60 * 1024 * 1024),
     )(extended, matrix, coef)
-    summed = part
-    for axis in axes:
-        summed = lax.psum_scatter(summed, axis, scatter_dimension=0, tiled=True)
-    return (summed[:, :columns], summed[:, columns:])
+    return tuple(reduced(part))
 
 
 def solution(mesh):

time: 221 us -> 150 us (0.68)
  waiting for transfers between devices: 109 us -> 28.5 us
  Pallas kernels: 36.3 us -> 57.5 us
  between operations: 14 us -> 0.86 us
    reduce_scatter x3 -> x0, waiting for transfers between devices: 80.9 us -> none  [per_device(): summed = lax.psum_scatter(summed, axis, scatter_dimension=0, tiled=True)]
    pallas_call x0 -> x1, Pallas kernels: none -> 21.2 us  [reduced(): pl.pallas_call(functools.partial(reduce_kernel, cut), out_shape=[jax.Shap...]
    unnamed x7 -> x9, local copies, waits for them, and re-layouts: 2.16 us -> 4.91 us
  transfers between devices with their start and end apart: 10 -> 7, of which waited for: 8 -> 5; matrix products, arithmetic and copies ran while one was open for 5% -> 7% of each run, Pallas kernels for 0% -> 0%
where the time goes in v2:
time: 150 us; the launch traced here: 149 us
  Pallas kernels  57.5 us (38%)
  local copies, waits for them, and re-layouts  41.7 us (28%)
  waiting for transfers between devices  28.5 us (19%)
  other arithmetic  11.1 us (7%)
  starting transfers between devices  9.02 us (6%)
    pallas_call x1, Pallas kernels, per_device(): pl.pallas_call(functools.partial(kernel, 0.5 / total_cells), out_shape=ja...  36.3 us
    concatenate x1, local copies, waits for them, and re-layouts, per_device(): jnp.concatenate([eigvecs.reshape(size_x, size_y * size_z, columns), y_fac...  30 us
    ppermute x7, waiting for transfers between devices, upper(): return lax.ppermute(head, axis, [(i + 1, i) for i in range(count - 1)])  28.5 us
    pallas_call x1, Pallas kernels, reduced(): pl.pallas_call(functools.partial(reduce_kernel, cut), out_shape=[jax.Shap...  21.2 us
    ppermute x7, starting transfers between devices, upper(): return lax.ppermute(head, axis, [(i + 1, i) for i in range(count - 1)])  9.02 us
    concatenate x1, other arithmetic, per_device(): extended = jnp.concatenate([plane, upper(plane, 'gx', 0)], axis=0)  6.96 us
    unnamed x9, local copies, waits for them, and re-layouts  4.91 us
    slice x3, local copies, waits for them, and re-layouts, upper(): head = lax.slice_in_dim(cells, 0, 1, axis=dim)  3.24 us
  transfers between devices with their start and end apart: 7, of which 5 were waited for; matrix products, arithmetic and copies ran while one was open for 7% of the time, Pallas kernels for 0%

profile of v2, /device:TPU:0, one launch (start us, length us, event | category | flops | bytes accessed | tf_op | source)
XLA Modules:
  0.0 148.7 jit_solution(17030912710084554528)
XLA Ops:
  0.6 0.9 copy.58
  1.6 1.3 collective-permute-start.4
  2.9 1.9 %collective-permute-done.4 = f32[2,16,8,1]{3,1,2,0:T(8,128)S(1)} collective-permute-done((f32[2,16,8,1]{3,1,2,0:T(8,128)S(1)}, f32[2,16,8,1]{3,1,2,0:T(8,128)S(1)}, u32[]{:S(2)}, u32[]{:S(2)}) %collective-permute-start.4) | collective-permute-done | bytes 1056 | tf_op jit(solution)/shard_map/ppermute | solution.py:14
  4.8 0.1 pad_maximum_fusion.3
  4.9 1.3 collective-permute-start.5
  6.2 5.3 %collective-permute-done.5 = f32[2,16,1,49]{3,1,2,0:T(8,128)S(1)} collective-permute-done((f32[2,16,1,49]{3,1,2,0:T(8,128)S(1)}, f32[2,16,1,49]{3,1,2,0:T(8,128)S(1)}, u32[]{:S(2)}, u32[]{:S(2)}) %collective-permute-start.5) | collective-permute-done | bytes 6304 | tf_op jit(solution)/shard_map/ppermute | solution.py:14
  11.5 0.1 pad_maximum_fusion.4
  11.5 1.3 collective-permute-start.6
  12.8 1.2 slice_bitcast_fusion
  14.0 1.3 collective-permute-start
  15.3 1.4 slice.52
  16.8 1.3 collective-permute-start.1
  18.1 0.0 collective-permute-done.6
  18.1 0.1 pad_maximum_fusion.2
  18.2 0.7 multiply_add_fusion
  19.0 1.1 collective-permute-done.1
  20.1 1.3 collective-permute-start.2
  21.4 0.7 fusion.1
  22.1 14.2 %collective-permute-done.2 = bf16[16,1,512]{2,1,0:T(2,128)(2,1)S(1)} collective-permute-done((bf16[16,1,512]{2,1,0:T(2,128)(2,1)S(1)}, bf16[16,1,512]{2,1,0:T(2,128)(2,1)S(1)}, u32[]{:S(2)}, u32[]{:S(2)}) %collective-permute-start.2) | collective-permute-done | bytes 16416 | tf_op jit(solution)/shard_map/ppermute | solution.py:14
  36.3 0.0 collective-permute-done
  36.3 0.0 copy-start
  36.3 0.0 copy-start.1
  36.3 30.0 %concatenate.18 = bf16[16,448,512]{2,1,0:T(8,128)(2,1)} concatenate(bf16[16,384,512]{2,1,0:T(8,128)(2,1)} %bitcast.19, bf16[16,48,512]{2,1,0:T(8,128)(2,1)S(1)} %bitcast.22, bf16[16,8,512]{2,1,0:T(8,128)(2,1)S(1)} %bitcast.24, bf16[16,1,512]{2,1,0:T(2,128)(2,1)S(1)} %collective-permute-done.2, bf16[16,7,512]{2,1,0:T(8,128)(2,1)S(1)} %broadcast_in_dim.3), dimensions={1} | concatenate | bytes 14680064 | tf_op jit(solution)/shard_map/concatenate | solution.py:229
  66.3 1.8 %slice.69 = bf16[1,448,512]{2,1,0:T(8,128)(2,1)} slice(bf16[16,448,512]{2,1,0:T(8,128)(2,1)} %concatenate.18), slice={[0:1], [0:448], [0:512]} | slice | bytes 917504 | tf_op jit(solution)/shard_map/slice | solution.py:13
  68.1 1.3 collective-permute-start.3
  69.4 0.0 copy-done
  69.4 0.0 copy-done.1
  69.4 0.1 add_bitcast_fusion
  69.5 0.6 copy.63
  70.2 0.6 copy.62
  70.8 0.6 copy.61
  71.4 1.5 pad_maximum_fusion.1
  72.9 0.3 slice.73
  73.2 1.2 copy.70
  74.4 0.2 reshape.40
  74.6 0.8 select_maximum_fusion.c_ref
  75.4 6.1 %collective-permute-done.3 = bf16[1,448,512]{2,1,0:T(8,128)(2,1)} collective-permute-done((bf16[1,448,512]{2,1,0:T(8,128)(2,1)}, bf16[1,448,512]{2,1,0:T(8,128)(2,1)}, u32[]{:S(2)}, u32[]{:S(2)}) %collective-permute-start.3) | collective-permute-done | bytes 458784 | tf_op jit(solution)/shard_map/ppermute | solution.py:14
  81.5 7.0 %pad_maximum_fusion.e_ref = bf16[17,448,512]{2,1,0:T(8,128)(2,1)} fusion(bf16[1,448,512]{2,1,0:T(8,128)(2,1)} %collective-permute-done.3, bf16[16,448,512]{2,1,0:T(8,128)(2,1)} %concatenate.18), kind=kLoop, calls=%fused_computation | loop fusion | flops 3899392 | bytes 15597568 | tf_op jit(solution)/shard_map/concatenate | solution.py:232
  88.5 36.3 %shard_map.86 = f32[512,1024]{1,0:T(8,128)} custom-call(bf16[17,448,512]{2,1,0:T(8,128)(2,1)} %pad_maximum_fusion.e_ref, bf16[896,448]{1,0:T(8,128)(2,1)} %constant.25.clone.t_ref, f32[17,8,448]{2,1,0:T(8,128)} %select_maximum_fusion.c_ref), custom_call_target="tpu_custom_call" | custom-call | tf_op jit(solution)/shard_map/pallas_call | solution.py:234
  124.7 21.2 %shard_map.87 = (f32[16,512]{1,0:T(8,128)}, f32[16,512]{1,0:T(8,128)}) custom-call(f32[4,4,2,16,1024]{4,3,2,1,0:T(8,128)} %bitcast.20), custom_call_target="tpu_custom_call" | custom-call | tf_op jit(solution)/shard_map/pallas_call | solution.py:192
  146.0 1.4 copy.76
  147.3 1.4 copy.77
  (5 shorter events, 0.1 us)
Async XLA Ops:
  1.6 3.2 %collective-permute-start.4 = (f32[2,16,8,1]{3,1,2,0:T(8,128)S(1)}, f32[2,16,8,1]{3,1,2,0:T(8,128)S(1)}, u32[]{:S(2)}, u32[]{:S(2)}) collective-permute-start(f32[2,16,8,1]{3,1,2,0:T(8,128)S(1)} %bitcast.21), channel_id=1, source_target_pairs={{1,0},{3,2},{5,4},{7,6},{9,8},{11,10},{13,12},{15,14},{17,16},{19,... | collective-permute-start | bytes 3080 | tf_op jit(solution)/shard_map/ppermute | solution.py:14
  4.9 6.6 %collective-permute-start.5 = (f32[2,16,1,49]{3,1,2,0:T(8,128)S(1)}, f32[2,16,1,49]{3,1,2,0:T(8,128)S(1)}, u32[]{:S(2)}, u32[]{:S(2)}) collective-permute-start(f32[2,16,1,49]{3,1,2,0:T(8,128)S(1)} %pad_maximum_fusion.3), channel_id=1, source_target_pairs={{2,0},{4,2},{6,4},{3,1},{5,3},{7,5},{10,8},{12,10},{14,12},{11,9},... | collective-permute-start | bytes 18824 | tf_op jit(solution)/shard_map/ppermute | solution.py:14
  11.5 6.5 %collective-permute-start.6 = (f32[2,1,9,49]{3,1,2,0:T(1,128)S(1)}, f32[2,1,9,49]{3,1,2,0:T(1,128)S(1)}, u32[]{:S(2)}, u32[]{:S(2)}) collective-permute-start(f32[2,1,9,49]{3,1,2,0:T(1,128)S(1)} %pad_maximum_fusion.4), channel_id=1, source_target_pairs={{8,0},{16,8},{24,16},{9,1},{17,9},{25,17},{10,2},{18,10},{26,18},{... | collective-permute-start | bytes 10592 | tf_op jit(solution)/shard_map/ppermute | solution.py:14
  14.0 22.2 %collective-permute-start = (bf16[16,1,48,512]{3,2,0,1:T(8,128)(2,1)S(1)}, bf16[16,1,48,512]{3,2,0,1:T(8,128)(2,1)S(1)}, u32[]{:S(2)}, u32[]{:S(2)}) collective-permute-start(bf16[16,1,48,512]{3,2,0,1:T(8,128)(2,1)S(1)} %slice_bitcast_fusion), channel_id=1, source_target_pairs={{2,0},{4,2},{6,4},{3,1},{5,3},{7,5},{10,8},{12,10},{14,12},{11,9},... | collective-permute-start | bytes 2359304 | tf_op jit(solution)/shard_map/ppermute | solution.py:14
  16.8 3.2 %collective-permute-start.1 = (bf16[16,8,1,512]{3,1,0,2:T(8,128)(2,1)S(1)}, bf16[16,8,1,512]{3,1,0,2:T(8,128)(2,1)S(1)}, u32[]{:S(2)}, u32[]{:S(2)}) collective-permute-start(bf16[16,8,1,512]{3,1,0,2:T(8,128)(2,1)S(1)} %copy.73), channel_id=1, source_target_pairs={{1,0},{3,2},{5,4},{7,6},{9,8},{11,10},{13,12},{15,14},{17,16},{19,... | collective-permute-start | bytes 393224 | tf_op jit(solution)/shard_map/ppermute | solution.py:14
  20.1 16.2 %collective-permute-start.2 = (bf16[16,1,512]{2,1,0:T(2,128)(2,1)S(1)}, bf16[16,1,512]{2,1,0:T(2,128)(2,1)S(1)}, u32[]{:S(2)}, u32[]{:S(2)}) collective-permute-start(bf16[16,1,512]{2,1,0:T(2,128)(2,1)S(1)} %slice.68), channel_id=1, source_target_pairs={{2,0},{4,2},{6,4},{3,1},{5,3},{7,5},{10,8},{12,10},{14,12},{11,9},... | collective-permute-start | bytes 49160 | tf_op jit(solution)/shard_map/ppermute | solution.py:14
  36.3 33.1 %copy-start = (f32[17,9,49]{2,0,1:T(8,128)S(1)}, f32[17,9,49]{2,0,1:T(8,128)}, u32[]{:S(2)}) copy-start(f32[17,9,49]{2,0,1:T(8,128)} %constant.24.clone) | copy-start | bytes 89968
  36.3 33.1 %copy-start.1 = (f32[49]{0:T(128)S(1)}, f32[49]{0:T(128)}, u32[]{:S(2)}) copy-start(f32[49]{0:T(128)} %constant.36) | copy-start | bytes 592
  68.1 13.4 %collective-permute-start.3 = (bf16[1,448,512]{2,1,0:T(8,128)(2,1)}, bf16[1,448,512]{2,1,0:T(8,128)(2,1)}, u32[]{:S(2)}, u32[]{:S(2)}) collective-permute-start(bf16[1,448,512]{2,1,0:T(8,128)(2,1)} %slice.69), channel_id=1, source_target_pairs={{8,0},{16,8},{24,16},{9,1},{17,9},{25,17},{10,2},{18,10},{26,18},{... | collective-permute-start | bytes 1376264 | tf_op jit(solution)/shard_map/ppermute | solution.py:14

commit v3 on v2

--- a/solution.py
+++ b/solution.py
@@ -22,9 +22,11 @@
 
 def rows_of(size_y, size_z):
     order = np.zeros((size_y + 1, size_z + 1), np.int64)
+    base = (size_y + 1) * size_z
     for y in range(size_y + 1):
         order[y, :size_z] = y * size_z + np.arange(size_z)
-        order[y, size_z] = (size_y + 1) * size_z + y
+        order[y, size_z] = base + y
+    order[size_y, size_z] = base + -(-size_y // 16) * 16
     return order
 
 
@@ -58,13 +60,85 @@
     diag = owned * kappa + field * (1.0 / 32.0)
     parts = jnp.stack([diag, kappa * (1.0 / 16.0), rho * (1.0 / 216.0)], axis=1)
     main = parts[..., :size_z].reshape(size_x + 1, 3, (size_y + 1) * size_z)
-    edge = parts[..., size_z]
-    both = jnp.concatenate([main, edge], axis=2)
+    edge = parts[:, :, :size_y, size_z]
+    edge = jnp.pad(edge, ((0, 0), (0, 0), (0, -size_y % 16)))
+    both = jnp.concatenate([main, edge, parts[:, :, size_y:, size_z]], axis=2)
     return jnp.pad(both, ((0, 0), (0, 5), (0, rows - both.shape[2])))
 
 
-def kernel(scale, e_ref, t_ref, c_ref, out_ref, pq, acc):
+OFFSETS = [(0, 1, 0), (0, 0, 1), (1, 0, 0), (0, 1, 1), (1, 0, 1), (1, 1, 0), (1, 1, 1)]
+AXES = ("gx", "gy", "gz")
+
+
+def inside(offset, sign):
+    ok = None
+    for axis, d in zip(AXES, offset):
+        if d:
+            at = lax.axis_index(axis)
+            here = at > 0 if sign < 0 else at < lax.axis_size(axis) - 1
+            ok = here if ok is None else jnp.logical_and(ok, here)
+    return ok
+
+
+def device_at(offset, sign):
+    return {axis: lax.axis_index(axis) + sign * d for axis, d in zip(AXES, offset) if d}
+
+
+def greet_around():
+    barrier = pltpu.get_barrier_semaphore()
+    total = jnp.int32(0)
+    for offset in OFFSETS:
+        for sign in (-1, 1):
+            there = inside(offset, sign)
+
+            @pl.when(there)
+            def _(offset=offset, sign=sign):
+                pl.semaphore_signal(barrier, inc=1, device_id=device_at(offset, sign),
+                                    device_id_type=pl.DeviceIdType.MESH)
+
+            total = total + jnp.where(there, 1, 0)
+    pl.semaphore_wait(barrier, total)
+
+
+def kernel(scale, v_ref, z_ref, k_ref, t_ref, c_ref, out_ref, e_ref, corners, pq, acc,
+           own_sem, send, recv):
     planes, rows, columns = e_ref.shape
+    nx, owned, _ = v_ref.shape
+    edge = z_ref.shape[1]
+    width = rows - owned - edge - 16
+    y_at, z_at, c_at = owned, owned + width, owned + width + edge
+    own = pltpu.make_async_copy(v_ref, e_ref.at[:nx, :owned], own_sem)
+    own.start()
+    places = {
+        (0, 1, 0): (v_ref.at[:, :width], e_ref.at[:nx, y_at:z_at]),
+        (0, 0, 1): (z_ref, e_ref.at[:nx, z_at:c_at]),
+        (0, 1, 1): (k_ref, corners.at[0]),
+        (1, 0, 0): (v_ref.at[0], e_ref.at[nx, :owned]),
+        (1, 0, 1): (z_ref.at[0], e_ref.at[nx, z_at:c_at]),
+        (1, 1, 0): (v_ref.at[0, :width], e_ref.at[nx, y_at:z_at]),
+        (1, 1, 1): (k_ref, corners.at[1]),
+    }
+    greet_around()
+    copies = {}
+    for n, offset in enumerate(OFFSETS):
+        src, dst = places[offset]
+        copies[offset] = pltpu.make_async_remote_copy(
+            src_ref=src, dst_ref=dst, send_sem=send.at[n], recv_sem=recv.at[n],
+            device_id=device_at(offset, -1), device_id_type=pl.DeviceIdType.MESH)
+        pl.when(inside(offset, -1))(copies[offset].start)
+    for offset in OFFSETS:
+        src, dst = places[offset]
+
+        @pl.when(jnp.logical_not(inside(offset, 1)))
+        def _(dst=dst):
+            dst[...] = jnp.zeros(dst.shape, dst.dtype)
+
+    own.wait()
+    for offset in OFFSETS:
+        pl.when(inside(offset, 1))(copies[offset].wait_recv)
+    for x in range(planes):
+        row = corners[0, x:x + 1] if x < nx else corners[1, 0:1]
+        e_ref[x, c_at:] = jnp.broadcast_to(row.astype(jnp.float32), (16, columns)).astype(e_ref.dtype)
 
     def taps_of(x):
         pq[lax.rem(x, 3)] = jnp.dot(t_ref[...], e_ref[x], preferred_element_type=jnp.float32)
@@ -102,6 +176,8 @@
     for half in range(2):
         m = acc[:, half * columns:(half + 1) * columns]
         out_ref[:, half * columns:(half + 1) * columns] = (m + m.T) * scale
+    for offset in OFFSETS:
+        pl.when(inside(offset, -1))(copies[offset].wait_send)
 
 
 def spread(axis, piece, landing, send, recv):
@@ -220,28 +296,31 @@
     ext = material
     for axis, dim in (("gz", 3), ("gy", 2), ("gx", 1)):
         ext = jnp.concatenate([ext, upper(ext, axis, dim)], axis=dim)
-    rows = -(-((size_y + 1) * (size_z + 1)) // 16) * 16
+    edge = -(-size_y // 16) * 16
+    rows = (size_y + 1) * size_z + edge + 16
     coef = coefficients(ext, rows, (size_x, size_y, size_z))
-    z_edge = upper(eigvecs, "gz", 2)[:, :, 0]
-    y_face = upper(eigvecs, "gy", 1)[:, 0]
-    y_edge = upper(z_edge, "gy", 1)
-    tail = rows - (size_y + 1) * (size_z + 1)
-    plane = jnp.concatenate(
-        [eigvecs.reshape(size_x, size_y * size_z, columns), y_face, z_edge, y_edge,
-         jnp.zeros((size_x, tail, columns), eigvecs.dtype)], axis=1)
-    extended = jnp.concatenate([plane, upper(plane, "gx", 0)], axis=0)
+    z_layer = jnp.pad(eigvecs[:, :, 0], ((0, 0), (0, edge - size_y), (0, 0)))
+    corner = eigvecs[:, 0, 0]
     matrix = jnp.asarray(plane_matrix(size_y, size_z, rows), jnp.bfloat16)
+    vmem = pl.BlockSpec(memory_space=pltpu.VMEM)
+    anywhere = pl.BlockSpec(memory_space=pl.ANY)
     part = pl.pallas_call(
         functools.partial(kernel, 0.5 / total_cells),
         out_shape=jax.ShapeDtypeStruct((columns, 2 * columns), jnp.float32),
-        in_specs=[pl.BlockSpec(memory_space=pltpu.VMEM)] * 3,
-        out_specs=pl.BlockSpec(memory_space=pltpu.VMEM),
+        in_specs=[anywhere, vmem, vmem, vmem, vmem],
+        out_specs=vmem,
         scratch_shapes=[
+            pltpu.VMEM((size_x + 1, rows, columns), eigvecs.dtype),
+            pltpu.VMEM((2, size_x, columns), eigvecs.dtype),
             pltpu.VMEM((3, 2 * rows, columns), jnp.float32),
             pltpu.VMEM((columns, 2 * columns), jnp.float32),
+            pltpu.SemaphoreType.DMA,
+            pltpu.SemaphoreType.DMA((7,)),
+            pltpu.SemaphoreType.DMA((7,)),
         ],
-        compiler_params=pltpu.CompilerParams(vmem_limit_bytes=60 * 1024 * 1024),
-    )(extended, matrix, coef)
+        compiler_params=pltpu.CompilerParams(
+            vmem_limit_bytes=60 * 1024 * 1024, collective_id=0, has_side_effects=True),
+    )(eigvecs.reshape(size_x, size_y * size_z, columns), z_layer, corner, matrix, coef)
     return tuple(reduced(part))
 
 

time: 150 us -> 110 us (0.73)
  local copies, waits for them, and re-layouts: 41.7 us -> 13.9 us
  Pallas kernels: 57.5 us -> 80.5 us
  waiting for transfers between devices: 28.5 us -> 7.86 us
  other arithmetic: 11.1 us -> 2.3 us
  starting transfers between devices: 9.02 us -> 4 us
    concatenate x1 -> x0, local copies, waits for them, and re-layouts: 30 us -> none  [per_device(): jnp.concatenate([eigvecs.reshape(size_x, size_y * size_z, columns), y_fac...]
    pallas_call x1, Pallas kernels: 36.3 us -> 57.3 us  [per_device(): pl.pallas_call(functools.partial(kernel, 0.5 / total_cells), out_shape=ja...]
    ppermute x7 -> x3, waiting for transfers between devices: 28.5 us -> 7.86 us  [upper(): return lax.ppermute(head, axis, [(i + 1, i) for i in range(count - 1)])]
    concatenate x2 -> x1, other arithmetic: 7.76 us -> 0.11 us  [coefficients(): both = jnp.concatenate([main, edge, parts[:, :, size_y:, size_z]], axis=2)]
    ppermute x7 -> x3, starting transfers between devices: 9.02 us -> 4 us  [upper(): return lax.ppermute(head, axis, [(i + 1, i) for i in range(count - 1)])]
    pallas_call x1, Pallas kernels: 21.2 us -> 23.2 us  [reduced(): pl.pallas_call(functools.partial(reduce_kernel, cut), out_shape=[jax.Shap...]
    unnamed x9 -> x13, local copies, waits for them, and re-layouts: 4.91 us -> 4.34 us
  transfers between devices with their start and end apart: 7 -> 3, of which waited for: 5 -> 3; matrix products, arithmetic and copies ran while one was open for 7% -> 3% of each run, Pallas kernels for 0% -> 0%
where the time goes in v3:
time: 110 us; the launch traced here: 109 us
  Pallas kernels  80.5 us (73%)
  local copies, waits for them, and re-layouts  13.9 us (13%)
  waiting for transfers between devices  7.86 us (7%)
  starting transfers between devices  4 us (4%)
  other arithmetic  2.3 us (2%)
    pallas_call x1, Pallas kernels, per_device(): pl.pallas_call(functools.partial(kernel, 0.5 / total_cells), out_shape=ja...  57.3 us
    pallas_call x1, Pallas kernels, reduced(): pl.pallas_call(functools.partial(reduce_kernel, cut), out_shape=[jax.Shap...  23.2 us
    ppermute x3, waiting for transfers between devices, upper(): return lax.ppermute(head, axis, [(i + 1, i) for i in range(count - 1)])  7.86 us
    unnamed x13, local copies, waits for them, and re-layouts  4.34 us
    ppermute x3, starting transfers between devices, upper(): return lax.ppermute(head, axis, [(i + 1, i) for i in range(count - 1)])  4 us
    reshape x2, local copies, waits for them, and re-layouts, coefficients(): main = parts[..., :size_z].reshape(size_x + 1, 3, (size_y + 1) * size_z)  2.22 us
  transfers between devices with their start and end apart: 3, of which 3 were waited for; matrix products, arithmetic and copies ran while one was open for 3% of the time, Pallas kernels for 0%

profile of v3, /device:TPU:0, one launch (start us, length us, event | category | flops | bytes accessed | tf_op | source)
XLA Modules:
  0.0 109.4 jit_solution(11307780758018420776)
XLA Ops:
  0.6 0.0 copy-start.2
  0.6 0.9 copy.68
  1.6 0.0 copy-start.1
  1.6 0.0 copy-start
  1.6 0.0 copy-start.3
  1.6 1.4 %collective-permute-start = (f32[2,16,8,1]{3,1,2,0:T(8,128)S(1)}, f32[2,16,8,1]{3,1,2,0:T(8,128)S(1)}, u32[]{:S(2)}, u32[]{:S(2)}) collective-permute-start(f32[2,16,8,1]{3,1,2,0:T(8,128)S(1)} %bitcast.24), channel_id=1, source_target_pairs={{1,0},{3,2},{5,4},{7,6},{9,8},{11,10},{13,12},{15,14},{17,16},{19,... | collective-permute-start | bytes 3080 | tf_op jit(solution)/shard_map/ppermute | solution.py:14
  3.1 1.9 %collective-permute-done = f32[2,16,8,1]{3,1,2,0:T(8,128)S(1)} collective-permute-done((f32[2,16,8,1]{3,1,2,0:T(8,128)S(1)}, f32[2,16,8,1]{3,1,2,0:T(8,128)S(1)}, u32[]{:S(2)}, u32[]{:S(2)}) %collective-permute-start) | collective-permute-done | bytes 1056 | tf_op jit(solution)/shard_map/ppermute | solution.py:14
  5.0 0.1 pad_maximum_fusion.3
  5.1 1.3 %collective-permute-start.1 = (f32[2,16,1,49]{3,1,2,0:T(8,128)S(1)}, f32[2,16,1,49]{3,1,2,0:T(8,128)S(1)}, u32[]{:S(2)}, u32[]{:S(2)}) collective-permute-start(f32[2,16,1,49]{3,1,2,0:T(8,128)S(1)} %pad_maximum_fusion.3), channel_id=1, source_target_pairs={{2,0},{4,2},{6,4},{3,1},{5,3},{7,5},{10,8},{12,10},{14,12},{11,9},... | collective-permute-start | bytes 18824 | tf_op jit(solution)/shard_map/ppermute | solution.py:14
  6.4 5.3 %collective-permute-done.1 = f32[2,16,1,49]{3,1,2,0:T(8,128)S(1)} collective-permute-done((f32[2,16,1,49]{3,1,2,0:T(8,128)S(1)}, f32[2,16,1,49]{3,1,2,0:T(8,128)S(1)}, u32[]{:S(2)}, u32[]{:S(2)}) %collective-permute-start.1) | collective-permute-done | bytes 6304 | tf_op jit(solution)/shard_map/ppermute | solution.py:14
  11.6 0.1 pad_maximum_fusion.4
  11.7 1.3 %collective-permute-start.2 = (f32[2,1,9,49]{3,1,2,0:T(1,128)S(1)}, f32[2,1,9,49]{3,1,2,0:T(1,128)S(1)}, u32[]{:S(2)}, u32[]{:S(2)}) collective-permute-start(f32[2,1,9,49]{3,1,2,0:T(1,128)S(1)} %pad_maximum_fusion.4), channel_id=1, source_target_pairs={{8,0},{16,8},{24,16},{9,1},{17,9},{25,17},{10,2},{18,10},{26,18},{... | collective-permute-start | bytes 10592 | tf_op jit(solution)/shard_map/ppermute | solution.py:14
  13.0 0.9 slice.49
  14.0 1.4 %slice.48 = bf16[16,8,1,512]{3,2,1,0:T(2,128)(2,1)S(1)} slice(bf16[16,8,48,512]{3,2,1,0:T(8,128)(2,1)} %param.7), slice={[0:16], [0:8], [0:1], [0:512]} | slice | bytes 262144 | tf_op jit(solution)/shard_map/slice | solution.py:302
  15.4 0.6 copy.89
  16.0 0.7 pad.24.z_ref
  16.7 0.6 collective-permute-done.2
  17.4 0.1 pad_maximum_fusion.1
  17.5 0.0 copy-done.2
  17.5 0.1 multiply_add_fusion
  17.6 0.0 copy-done.1
  17.6 0.1 fusion.3
  17.7 0.0 copy-done
  17.7 0.0 copy-done.3
  17.7 0.1 add_bitcast_fusion
  17.9 0.6 copy.71
  18.5 0.6 copy.72
  19.1 0.6 copy.73
  19.7 0.1 pad_maximum_fusion.2
  19.9 1.5 %pad_maximum_fusion = f32[17,3,9,49]{2,1,0,3:T(4,128)S(1)} fusion(f32[17,1,9,49]{2,1,0,3:T(1,128)S(1)} %copy.73, f32[17,1,9,49]{2,1,0,3:T(1,128)S(1)} %copy.72, f32[17,1,9,49]{2,1,0,3:T(1,128)S(1)} %copy.71), kind=kLoop, calls=%fused_computation | loop fusion | flops 44982 | bytes 179928 | tf_op jit(solution)/shard_map/stack | solution.py:61
  21.4 0.1 copy.75
  21.5 0.1 copy.77
  21.6 1.5 %slice.67 = f32[17,3,9,48]{2,1,0,3:T(4,128)} slice(f32[17,3,9,49]{2,1,0,3:T(4,128)S(1)} %pad_maximum_fusion), slice={[0:17], [0:3], [0:9], [0:48]} | slice | bytes 176256 | tf_op jit(solution)/shard_map/slice | solution.py:62
  23.1 2.0 %copy.82 = f32[17,3,9,48]{3,2,1,0:T(8,128)S(1)} copy(f32[17,3,9,48]{2,1,0,3:T(4,128)} %slice.67) | data formatting | bytes 176256 | tf_op jit(solution)/shard_map/reshape | solution.py:62
  25.1 0.2 reshape.40
  25.3 0.1 fusion
  25.4 0.7 pad.29.c_ref
  26.2 57.3 %shard_map.86 = f32[512,1024]{1,0:T(8,128)} custom-call(bf16[16,384,512]{2,1,0:T(8,128)(2,1)} %bitcast.23, bf16[16,16,512]{2,1,0:T(8,128)(2,1)} %pad.24.z_ref, bf16[16,512]{1,0:T(8,128)(2,1)} %bitcast.26, bf16[928,464]{1,0:T(8,128)(2,1)} %constant.25.clone.t_ref, f32[17,8,464]{2,1,0:T(8,128)} %pad.29.c_ref), custom_call_target="tpu_custom_call" | custom-call | tf_op jit(solution)/shard_map/pallas_call | solution.py:307
  83.5 23.2 %shard_map.87 = (f32[16,512]{1,0:T(8,128)}, f32[16,512]{1,0:T(8,128)}) custom-call(f32[4,4,2,16,1024]{4,3,2,1,0:T(8,128)} %bitcast.22), custom_call_target="tpu_custom_call" | custom-call | tf_op jit(solution)/shard_map/pallas_call | solution.py:268
  106.7 1.4 %copy.92 = f32[16,512]{1,0:T(8,128)} copy(f32[16,512]{1,0:T(8,128)} %get-tuple-element.7) | data formatting | bytes 65536
  108.1 1.4 %copy.93 = f32[16,512]{1,0:T(8,128)} copy(f32[16,512]{1,0:T(8,128)} %get-tuple-element.8) | data formatting | bytes 65536
  (3 shorter events, 0.1 us)
Async XLA Ops:
  0.6 16.9 %copy-start.2 = (f32[17]{0:T(128)S(1)}, f32[17]{0:T(128)}, u32[]{:S(2)}) copy-start(f32[17]{0:T(128)} %constant.38) | copy-start | bytes 208
  1.6 16.0 %copy-start.1 = (f32[9]{0:T(128)S(1)}, f32[9]{0:T(128)}, u32[]{:S(2)}) copy-start(f32[9]{0:T(128)} %constant.39) | copy-start | bytes 112
  1.6 16.1 %copy-start = (f32[17,9,49]{2,0,1:T(8,128)S(1)}, f32[17,9,49]{2,0,1:T(8,128)}, u32[]{:S(2)}) copy-start(f32[17,9,49]{2,0,1:T(8,128)} %constant.24.clone) | copy-start | bytes 89968
  1.6 16.1 %copy-start.3 = (f32[49]{0:T(128)S(1)}, f32[49]{0:T(128)}, u32[]{:S(2)}) copy-start(f32[49]{0:T(128)} %constant.40) | copy-start | bytes 592
  1.6 3.4 %collective-permute-start = (f32[2,16,8,1]{3,1,2,0:T(8,128)S(1)}, f32[2,16,8,1]{3,1,2,0:T(8,128)S(1)}, u32[]{:S(2)}, u32[]{:S(2)}) collective-permute-start(f32[2,16,8,1]{3,1,2,0:T(8,128)S(1)} %bitcast.24), channel_id=1, source_target_pairs={{1,0},{3,2},{5,4},{7,6},{9,8},{11,10},{13,12},{15,14},{17,16},{19,... | collective-permute-start | bytes 3080 | tf_op jit(solution)/shard_map/ppermute | solution.py:14
  5.1 6.6 %collective-permute-start.1 = (f32[2,16,1,49]{3,1,2,0:T(8,128)S(1)}, f32[2,16,1,49]{3,1,2,0:T(8,128)S(1)}, u32[]{:S(2)}, u32[]{:S(2)}) collective-permute-start(f32[2,16,1,49]{3,1,2,0:T(8,128)S(1)} %pad_maximum_fusion.3), channel_id=1, source_target_pairs={{2,0},{4,2},{6,4},{3,1},{5,3},{7,5},{10,8},{12,10},{14,12},{11,9},... | collective-permute-start | bytes 18824 | tf_op jit(solution)/shard_map/ppermute | solution.py:14
  11.7 5.6 %collective-permute-start.2 = (f32[2,1,9,49]{3,1,2,0:T(1,128)S(1)}, f32[2,1,9,49]{3,1,2,0:T(1,128)S(1)}, u32[]{:S(2)}, u32[]{:S(2)}) collective-permute-start(f32[2,1,9,49]{3,1,2,0:T(1,128)S(1)} %pad_maximum_fusion.4), channel_id=1, source_target_pairs={{8,0},{16,8},{24,16},{9,1},{17,9},{25,17},{10,2},{18,10},{26,18},{... | collective-permute-start | bytes 10592 | tf_op jit(solution)/shard_map/ppermute | solution.py:14

commit v4 on v3

--- a/solution.py
+++ b/solution.py
@@ -100,10 +100,12 @@
     pl.semaphore_wait(barrier, total)
 
 
-def kernel(scale, v_ref, z_ref, k_ref, t_ref, c_ref, out_ref, e_ref, corners, pq, acc,
+def kernel(scale, v_ref, z_ref, k_ref, t_ref, c_ref, out_ref, e_ref, corners, p0, p1, p2, p3, acc,
            own_sem, send, recv):
-    planes, rows, columns = e_ref.shape
+    slots = (p0, p1, p2, p3)
+    rows, columns = e_ref.shape[1:]
     nx, owned, _ = v_ref.shape
+    planes = nx + 1
     edge = z_ref.shape[1]
     width = rows - owned - edge - 16
     y_at, z_at, c_at = owned, owned + width, owned + width + edge
@@ -140,39 +142,39 @@
         row = corners[0, x:x + 1] if x < nx else corners[1, 0:1]
         e_ref[x, c_at:] = jnp.broadcast_to(row.astype(jnp.float32), (16, columns)).astype(e_ref.dtype)
 
-    def taps_of(x):
-        pq[lax.rem(x, 3)] = jnp.dot(t_ref[...], e_ref[x], preferred_element_type=jnp.float32)
-
-    acc[...] = jnp.zeros_like(acc)
-    pq[2] = jnp.zeros(pq.shape[1:], jnp.float32)
-    taps_of(0)
-
-    def step(x, carry):
-        now, after, before = lax.rem(x, 3), lax.rem(x + 1, 3), lax.rem(x + 2, 3)
-
-        @pl.when(x < planes - 1)
-        def _():
-            taps_of(x + 1)
-
-        @pl.when(x == planes - 1)
-        def _():
-            pq[after] = jnp.zeros(pq.shape[1:], jnp.float32)
-
-        last = x == planes - 1
-        two = jnp.where(last, 0.0, 2.0)
-        four = jnp.where(last, 0.0, 4.0)
+    def taps_of(x, slot):
+        slots[slot % 4][...] = jnp.dot(t_ref[...], e_ref[x], preferred_element_type=jnp.float32)
+
+    def step(x, slot, two, four, ahead):
+        if ahead:
+            taps_of(x + 2, slot + 2)
+        before, now, after = (slots[(slot + k) % 4] for k in (3, 0, 1))
         coef = c_ref[x].T
         v = e_ref[x]
-        stiff = pq[before, :rows] + pq[after, :rows] + two * pq[now, :rows]
+        stiff = before[:rows] + after[:rows] + two * now[:rows]
         yk = coef[:, 0:1] * v.astype(jnp.float32) - coef[:, 1:2] * stiff
-        mass = pq[before, rows:] + pq[after, rows:] + four * pq[now, rows:]
+        mass = before[rows:] + after[rows:] + four * now[rows:]
         ym = coef[:, 2:3] * mass
         dims = (((0,), (0,)), ((), ()))
         acc[:, :columns] += lax.dot_general(v, yk.astype(jnp.bfloat16), dims, preferred_element_type=jnp.float32)
         acc[:, columns:] += lax.dot_general(v, ym.astype(jnp.bfloat16), dims, preferred_element_type=jnp.float32)
+
+    acc[...] = jnp.zeros_like(acc)
+    e_ref[planes] = jnp.zeros((rows, columns), e_ref.dtype)
+    p3[...] = jnp.zeros_like(p3)
+    taps_of(0, 0)
+    taps_of(1, 1)
+    whole = (planes - 1) // 4
+
+    def four_steps(i, carry):
+        for j in range(4):
+            step(4 * i + j, j, 2.0, 4.0, True)
         return carry
 
-    lax.fori_loop(0, planes, step, 0)
+    lax.fori_loop(0, whole, four_steps, 0)
+    for x in range(4 * whole, planes):
+        last = x == planes - 1
+        step(x, x, 0.0 if last else 2.0, 0.0 if last else 4.0, x + 2 <= planes)
     for half in range(2):
         m = acc[:, half * columns:(half + 1) * columns]
         out_ref[:, half * columns:(half + 1) * columns] = (m + m.T) * scale
@@ -310,9 +312,9 @@
         in_specs=[anywhere, vmem, vmem, vmem, vmem],
         out_specs=vmem,
         scratch_shapes=[
-            pltpu.VMEM((size_x + 1, rows, columns), eigvecs.dtype),
+            pltpu.VMEM((size_x + 2, rows, columns), eigvecs.dtype),
             pltpu.VMEM((2, size_x, columns), eigvecs.dtype),
-            pltpu.VMEM((3, 2 * rows, columns), jnp.float32),
+        ] + [pltpu.VMEM((2 * rows, columns), jnp.float32)] * 4 + [
             pltpu.VMEM((columns, 2 * columns), jnp.float32),
             pltpu.SemaphoreType.DMA,
             pltpu.SemaphoreType.DMA((7,)),

time: 110 us -> 102 us (0.927)
  Pallas kernels: 80.5 us -> 73 us
    pallas_call x1, Pallas kernels: 57.3 us -> 49.8 us  [per_device(): pl.pallas_call(functools.partial(kernel, 0.5 / total_cells), out_shape=ja...]
  transfers between devices with their start and end apart: 3 -> 3, of which waited for: 3 -> 3; matrix products, arithmetic and copies ran while one was open for 3% -> 4% of each run, Pallas kernels for 0% -> 0%
where the time goes in v4:
time: 102 us
  Pallas kernels  73 us (72%)
  local copies, waits for them, and re-layouts  13.9 us (14%)
  waiting for transfers between devices  7.86 us (8%)
  starting transfers between devices  4 us (4%)
  other arithmetic  2.3 us (2%)
    pallas_call x1, Pallas kernels, per_device(): pl.pallas_call(functools.partial(kernel, 0.5 / total_cells), out_shape=ja...  49.8 us
    pallas_call x1, Pallas kernels, reduced(): pl.pallas_call(functools.partial(reduce_kernel, cut), out_shape=[jax.Shap...  23.2 us
    ppermute x3, waiting for transfers between devices, upper(): return lax.ppermute(head, axis, [(i + 1, i) for i in range(count - 1)])  7.86 us
    unnamed x13, local copies, waits for them, and re-layouts  4.34 us
    ppermute x3, starting transfers between devices, upper(): return lax.ppermute(head, axis, [(i + 1, i) for i in range(count - 1)])  4 us
    reshape x2, local copies, waits for them, and re-layouts, coefficients(): main = parts[..., :size_z].reshape(size_x + 1, 3, (size_y + 1) * size_z)  2.22 us
  transfers between devices with their start and end apart: 3, of which 3 were waited for; matrix products, arithmetic and copies ran while one was open for 4% of the time, Pallas kernels for 0%

profile of v4, /device:TPU:0, one launch (start us, length us, event | category | flops | bytes accessed | tf_op | source)
XLA Modules:
  0.0 101.9 jit_solution(18308067895753995519)
XLA Ops:
  0.6 0.0 copy-start.2
  0.6 0.9 copy.68
  1.6 0.0 copy-start.1
  1.6 0.0 copy-start
  1.6 0.0 copy-start.3
  1.6 1.4 %collective-permute-start = (f32[2,16,8,1]{3,1,2,0:T(8,128)S(1)}, f32[2,16,8,1]{3,1,2,0:T(8,128)S(1)}, u32[]{:S(2)}, u32[]{:S(2)}) collective-permute-start(f32[2,16,8,1]{3,1,2,0:T(8,128)S(1)} %bitcast.24), channel_id=1, source_target_pairs={{1,0},{3,2},{5,4},{7,6},{9,8},{11,10},{13,12},{15,14},{17,16},{19,... | collective-permute-start | bytes 3080 | tf_op jit(solution)/shard_map/ppermute | solution.py:14
  3.1 1.9 %collective-permute-done = f32[2,16,8,1]{3,1,2,0:T(8,128)S(1)} collective-permute-done((f32[2,16,8,1]{3,1,2,0:T(8,128)S(1)}, f32[2,16,8,1]{3,1,2,0:T(8,128)S(1)}, u32[]{:S(2)}, u32[]{:S(2)}) %collective-permute-start) | collective-permute-done | bytes 1056 | tf_op jit(solution)/shard_map/ppermute | solution.py:14
  5.0 0.1 pad_maximum_fusion.3
  5.1 1.3 %collective-permute-start.1 = (f32[2,16,1,49]{3,1,2,0:T(8,128)S(1)}, f32[2,16,1,49]{3,1,2,0:T(8,128)S(1)}, u32[]{:S(2)}, u32[]{:S(2)}) collective-permute-start(f32[2,16,1,49]{3,1,2,0:T(8,128)S(1)} %pad_maximum_fusion.3), channel_id=1, source_target_pairs={{2,0},{4,2},{6,4},{3,1},{5,3},{7,5},{10,8},{12,10},{14,12},{11,9},... | collective-permute-start | bytes 18824 | tf_op jit(solution)/shard_map/ppermute | solution.py:14
  6.4 5.3 %collective-permute-done.1 = f32[2,16,1,49]{3,1,2,0:T(8,128)S(1)} collective-permute-done((f32[2,16,1,49]{3,1,2,0:T(8,128)S(1)}, f32[2,16,1,49]{3,1,2,0:T(8,128)S(1)}, u32[]{:S(2)}, u32[]{:S(2)}) %collective-permute-start.1) | collective-permute-done | bytes 6304 | tf_op jit(solution)/shard_map/ppermute | solution.py:14
  11.6 0.1 pad_maximum_fusion.4
  11.7 1.3 %collective-permute-start.2 = (f32[2,1,9,49]{3,1,2,0:T(1,128)S(1)}, f32[2,1,9,49]{3,1,2,0:T(1,128)S(1)}, u32[]{:S(2)}, u32[]{:S(2)}) collective-permute-start(f32[2,1,9,49]{3,1,2,0:T(1,128)S(1)} %pad_maximum_fusion.4), channel_id=1, source_target_pairs={{8,0},{16,8},{24,16},{9,1},{17,9},{25,17},{10,2},{18,10},{26,18},{... | collective-permute-start | bytes 10592 | tf_op jit(solution)/shard_map/ppermute | solution.py:14
  13.0 0.9 slice.49
  14.0 1.4 %slice.48 = bf16[16,8,1,512]{3,2,1,0:T(2,128)(2,1)S(1)} slice(bf16[16,8,48,512]{3,2,1,0:T(8,128)(2,1)} %param.7), slice={[0:16], [0:8], [0:1], [0:512]} | slice | bytes 262144 | tf_op jit(solution)/shard_map/slice | solution.py:304
  15.4 0.6 copy.89
  16.0 0.7 pad.24.z_ref
  16.7 0.6 collective-permute-done.2
  17.4 0.1 pad_maximum_fusion.1
  17.5 0.0 copy-done.2
  17.5 0.1 multiply_add_fusion
  17.6 0.0 copy-done.1
  17.6 0.1 fusion.3
  17.7 0.0 copy-done
  17.7 0.0 copy-done.3
  17.7 0.1 add_bitcast_fusion
  17.9 0.6 copy.71
  18.5 0.6 copy.72
  19.1 0.6 copy.73
  19.7 0.1 pad_maximum_fusion.2
  19.9 1.5 %pad_maximum_fusion = f32[17,3,9,49]{2,1,0,3:T(4,128)S(1)} fusion(f32[17,1,9,49]{2,1,0,3:T(1,128)S(1)} %copy.73, f32[17,1,9,49]{2,1,0,3:T(1,128)S(1)} %copy.72, f32[17,1,9,49]{2,1,0,3:T(1,128)S(1)} %copy.71), kind=kLoop, calls=%fused_computation | loop fusion | flops 44982 | bytes 179928 | tf_op jit(solution)/shard_map/stack | solution.py:61
  21.4 0.1 copy.75
  21.5 0.1 copy.77
  21.6 1.5 %slice.67 = f32[17,3,9,48]{2,1,0,3:T(4,128)} slice(f32[17,3,9,49]{2,1,0,3:T(4,128)S(1)} %pad_maximum_fusion), slice={[0:17], [0:3], [0:9], [0:48]} | slice | bytes 176256 | tf_op jit(solution)/shard_map/slice | solution.py:62
  23.1 2.0 %copy.82 = f32[17,3,9,48]{3,2,1,0:T(8,128)S(1)} copy(f32[17,3,9,48]{2,1,0,3:T(4,128)} %slice.67) | data formatting | bytes 176256 | tf_op jit(solution)/shard_map/reshape | solution.py:62
  25.1 0.2 reshape.40
  25.3 0.1 fusion
  25.4 0.7 pad.29.c_ref
  26.2 49.8 %shard_map.86 = f32[512,1024]{1,0:T(8,128)} custom-call(bf16[16,384,512]{2,1,0:T(8,128)(2,1)} %bitcast.23, bf16[16,16,512]{2,1,0:T(8,128)(2,1)} %pad.24.z_ref, bf16[16,512]{1,0:T(8,128)(2,1)} %bitcast.26, bf16[928,464]{1,0:T(8,128)(2,1)} %constant.25.clone.t_ref, f32[17,8,464]{2,1,0:T(8,128)} %pad.29.c_ref), custom_call_target="tpu_custom_call" | custom-call | tf_op jit(solution)/shard_map/pallas_call | solution.py:309
  75.9 23.2 %shard_map.87 = (f32[16,512]{1,0:T(8,128)}, f32[16,512]{1,0:T(8,128)}) custom-call(f32[4,4,2,16,1024]{4,3,2,1,0:T(8,128)} %bitcast.22), custom_call_target="tpu_custom_call" | custom-call | tf_op jit(solution)/shard_map/pallas_call | solution.py:270
  99.1 1.4 %copy.92 = f32[16,512]{1,0:T(8,128)} copy(f32[16,512]{1,0:T(8,128)} %get-tuple-element.7) | data formatting | bytes 65536
  100.5 1.4 %copy.93 = f32[16,512]{1,0:T(8,128)} copy(f32[16,512]{1,0:T(8,128)} %get-tuple-element.8) | data formatting | bytes 65536
  (3 shorter events, 0.1 us)
Async XLA Ops:
  0.6 16.9 %copy-start.2 = (f32[17]{0:T(128)S(1)}, f32[17]{0:T(128)}, u32[]{:S(2)}) copy-start(f32[17]{0:T(128)} %constant.38) | copy-start | bytes 208
  1.6 16.0 %copy-start.1 = (f32[9]{0:T(128)S(1)}, f32[9]{0:T(128)}, u32[]{:S(2)}) copy-start(f32[9]{0:T(128)} %constant.39) | copy-start | bytes 112
  1.6 16.1 %copy-start = (f32[17,9,49]{2,0,1:T(8,128)S(1)}, f32[17,9,49]{2,0,1:T(8,128)}, u32[]{:S(2)}) copy-start(f32[17,9,49]{2,0,1:T(8,128)} %constant.24.clone) | copy-start | bytes 89968
  1.6 16.1 %copy-start.3 = (f32[49]{0:T(128)S(1)}, f32[49]{0:T(128)}, u32[]{:S(2)}) copy-start(f32[49]{0:T(128)} %constant.40) | copy-start | bytes 592
  1.6 3.4 %collective-permute-start = (f32[2,16,8,1]{3,1,2,0:T(8,128)S(1)}, f32[2,16,8,1]{3,1,2,0:T(8,128)S(1)}, u32[]{:S(2)}, u32[]{:S(2)}) collective-permute-start(f32[2,16,8,1]{3,1,2,0:T(8,128)S(1)} %bitcast.24), channel_id=1, source_target_pairs={{1,0},{3,2},{5,4},{7,6},{9,8},{11,10},{13,12},{15,14},{17,16},{19,... | collective-permute-start | bytes 3080 | tf_op jit(solution)/shard_map/ppermute | solution.py:14
  5.1 6.6 %collective-permute-start.1 = (f32[2,16,1,49]{3,1,2,0:T(8,128)S(1)}, f32[2,16,1,49]{3,1,2,0:T(8,128)S(1)}, u32[]{:S(2)}, u32[]{:S(2)}) collective-permute-start(f32[2,16,1,49]{3,1,2,0:T(8,128)S(1)} %pad_maximum_fusion.3), channel_id=1, source_target_pairs={{2,0},{4,2},{6,4},{3,1},{5,3},{7,5},{10,8},{12,10},{14,12},{11,9},... | collective-permute-start | bytes 18824 | tf_op jit(solution)/shard_map/ppermute | solution.py:14
  11.7 5.6 %collective-permute-start.2 = (f32[2,1,9,49]{3,1,2,0:T(1,128)S(1)}, f32[2,1,9,49]{3,1,2,0:T(1,128)S(1)}, u32[]{:S(2)}, u32[]{:S(2)}) collective-permute-start(f32[2,1,9,49]{3,1,2,0:T(1,128)S(1)} %pad_maximum_fusion.4), channel_id=1, source_target_pairs={{8,0},{16,8},{24,16},{9,1},{17,9},{25,17},{10,2},{18,10},{26,18},{... | collective-permute-start | bytes 10592 | tf_op jit(solution)/shard_map/ppermute | solution.py:14
